TPU v7x, 32 devices: a whole 2x2x4 slice. The times are simulated.
32 devices in a mesh: seq: 8 (over z, y), samp: 4 (over x, core).
Axes of the slice: x: 2, y: 2, z: 4, core: 2. Of those that a mesh axis runs over, the one named last changes fastest.
Arguments:
- queries: bfloat16 [4, 1024, 5120], P('samp', 'seq'), may hold values from -120 to 120
- prefix_keys: bfloat16 [1024, 1024], P('seq'), may hold values from -4 to 4
- prefix_values: bfloat16 [1024, 1024], P('seq'), may hold values from -4 to 4
- suffix_keys: bfloat16 [4, 1024, 1024], P('samp', 'seq'), may hold values from -5 to 5
- suffix_values: bfloat16 [4, 1024, 1024], P('samp', 'seq'), may hold values from -4 to 4
- layout_pre: int32 [4, 8, 8], P('samp', 'seq'), may hold values 0 or 1
- layout_suf: int32 [4, 8, 8], P('samp', 'seq'), may hold values 0 or 1
- lengths: int32 [4], P('samp'), may hold values from 1 to 8
Outputs:
- attended: bfloat16 [4, 1024, 5120], P('samp', 'seq')
All inputs are finite; a program needn't handle non-finite values. No bound on the sum of `layout_pre` or of `layout_suf` on one device may be relied on, other than what follows from the above.
Results may differ from a plain program's by a relative error of at most 0.004.
Values may be sent and summed in bfloat16 or wider, within the bound.
No kernel may reach another device: no remote copies, remote signals or barrier semaphores. Data moves between devices by JAX's collectives and lax.ppermute only.
A program may use at most 128 MiB of HBM per device.

v0:
```python
import math

import jax
import jax.numpy as jnp
from jax import lax
from jax.sharding import PartitionSpec as P

HEADS = 40
KV_HEADS = 8
HEAD_DIM = 128
BLOCK = 128


masked_value = -1e30


def block_size(count):
    return math.gcd(count, 512)


def softmax_step(carry, scores, allowed, value_rows, form):
    run_max, run_sum, run_total = carry
    key_mask = allowed[:, None, None, :, :]
    block_max = jnp.max(jnp.where(key_mask, scores, masked_value), axis=-1)
    new_max = jnp.maximum(run_max, block_max)
    weights = jnp.where(key_mask, jnp.exp(scores - new_max[..., None]), 0.0)
    scale_old = jnp.exp(run_max - new_max)
    new_sum = run_sum * scale_old + jnp.sum(weights, axis=-1)
    rounded = weights.astype(jnp.bfloat16)
    added = jnp.einsum(form, rounded, value_rows, preferred_element_type=jnp.float32)
    rescale = jnp.transpose(scale_old, (0, 3, 1, 2))[..., None]
    return (new_max, new_sum, run_total * rescale + added)


def lookup(table, block_ids):
    columns = jnp.arange(table.shape[1], dtype=jnp.int32)
    onehot = (block_ids[None, :] == columns[:, None]).astype(jnp.int32)
    return jnp.sum(table[:, :, None] * onehot[None, :, :], axis=1) > 0


def shards(
    queries, prefix_keys, prefix_values, suffix_keys, suffix_values, layout_pre, layout_suf, lengths
):
    group_size = HEADS // KV_HEADS
    score_scale = 1.0 / math.sqrt(HEAD_DIM)
    samples = queries.shape[0]
    query_block = lax.axis_index("seq")
    query_grid = queries.reshape(samples, BLOCK, KV_HEADS, group_size, HEAD_DIM)
    query_position = query_block * BLOCK + jnp.arange(BLOCK, dtype=jnp.int32)
    pre_table = layout_pre[:, 0, :]
    suf_table = layout_suf[:, 0, :]
    start_carry = (
        jnp.full((samples, KV_HEADS, group_size, BLOCK), masked_value, jnp.float32),
        jnp.zeros((samples, KV_HEADS, group_size, BLOCK), jnp.float32),
        jnp.zeros((samples, BLOCK, KV_HEADS, group_size, HEAD_DIM), jnp.float32),
    )
    share = prefix_keys.shape[0] // lax.axis_size("samp")
    seq_count = lax.axis_size("seq")
    shard_rows = prefix_keys.shape[0]
    share_start = lax.axis_index("samp") * share
    own_keys = lax.dynamic_slice_in_dim(prefix_keys, share_start, share, 0)
    own_values = lax.dynamic_slice_in_dim(prefix_values, share_start, share, 0)
    shares = (
        lax.all_gather(own_keys, "seq", axis=0, tiled=True),
        lax.all_gather(own_values, "seq", axis=0, tiled=True),
    )
    pieces = (
        lax.all_gather(shares[0], "samp", axis=0, tiled=True),
        lax.all_gather(shares[1], "samp", axis=0, tiled=True),
    )
    whole_index = jnp.arange(pieces[0].shape[0], dtype=jnp.int32)
    owner_share = whole_index // (seq_count * share)
    remainder = whole_index % (seq_count * share)
    positions = remainder // share * shard_rows + owner_share * share + remainder % share
    carry = start_carry
    key_rows = pieces[0]
    value_rows = pieces[1]
    count = key_rows.shape[0]
    prefix_size = block_size(count)
    steps = count // prefix_size

    def prefix_one_step(inner, pieces):
        key_part, value_part, place = pieces
        key_grid = key_part.reshape(prefix_size, KV_HEADS, HEAD_DIM)
        value_grid = value_part.reshape(prefix_size, KV_HEADS, HEAD_DIM)
        scores = (
            jnp.einsum("sqgjd,rgd->sgjqr", query_grid, key_grid, preferred_element_type=jnp.float32)
            * score_scale
        )
        seen = lookup(pre_table, place // BLOCK)
        allowed = jnp.broadcast_to(seen[:, None, :], (samples, BLOCK, prefix_size))
        return (softmax_step(inner, scores, allowed, value_grid, "sgjqr,rgd->sqgjd"), None)

    width = key_rows.shape[1]
    carry, unused = lax.scan(
        prefix_one_step,
        carry,
        (
            key_rows.reshape(steps, prefix_size, width),
            value_rows.reshape(steps, prefix_size, width),
            positions.reshape(steps, prefix_size),
        ),
    )
    suffix_carry = carry
    key_rows = lax.all_gather(suffix_keys, "seq", axis=1, tiled=True)
    value_rows = lax.all_gather(suffix_values, "seq", axis=1, tiled=True)
    count = key_rows.shape[1]
    size = block_size(count)
    steps = count // size
    width = key_rows.shape[2]
    positions = jnp.arange(count, dtype=jnp.int32).reshape(steps, size)

    def suffix_one_step(inner, items):
        key_part, value_part, place = items
        key_grid = key_part.reshape(samples, size, KV_HEADS, HEAD_DIM)
        value_grid = value_part.reshape(samples, size, KV_HEADS, HEAD_DIM)
        scores = (
            jnp.einsum(
                "sqgjd,srgd->sgjqr", query_grid, key_grid, preferred_element_type=jnp.float32
            )
            * score_scale
        )
        key_block = place // BLOCK
        block_seen = (key_block == query_block)[None, :] | lookup(suf_table, key_block)
        causal = place[None, :] <= query_position[:, None]
        allowed = block_seen[:, None, :] & causal[None, :, :]
        return (softmax_step(inner, scores, allowed, value_grid, "sgjqr,srgd->sqgjd"), None)

    key_steps = jnp.transpose(key_rows.reshape(samples, steps, size, width), (1, 0, 2, 3))
    value_steps = jnp.transpose(value_rows.reshape(samples, steps, size, width), (1, 0, 2, 3))
    suffix_carry, unused = lax.scan(
        suffix_one_step, suffix_carry, (key_steps, value_steps, positions)
    )
    carry = suffix_carry
    run_max, run_sum, run_total = carry
    mixed = run_total / jnp.transpose(run_sum, (0, 3, 1, 2))[..., None]
    mixed = mixed.reshape(samples, BLOCK, HEADS * HEAD_DIM)
    is_live = (query_block < lengths)[:, None, None]
    return jnp.where(is_live, mixed, 0.0).astype(jnp.bfloat16)


def solution(mesh):
    return jax.shard_map(
        shards,
        mesh=mesh,
        in_specs=(
            P("samp", "seq", None),
            P("seq", None),
            P("seq", None),
            P("samp", "seq", None),
            P("samp", "seq", None),
            P("samp", "seq", None),
            P("samp", "seq", None),
            P("samp"),
        ),
        out_specs=P("samp", "seq", None),
        check_vma=False,
    )
```

profile of v0, /device:TPU:0, one launch (start us, length us, event | category | flops | bytes accessed | tf_op | source)
XLA Modules:
  0.0 262.5 jit_solution(15586592918994311306)
XLA Ops:
  6.5 0.9 copy-done
  7.5 35.3 %all_gather.18 = bf16[256,1024]{1,0:T(8,128)(2,1)} all-gather(bf16[32,1024]{1,0:T(8,128)(2,1)S(1)} %constant_dynamic-slice_fusion.6), channel_id=1, replica_groups=mesh['seq'=8,'samp'=4] {'seq'}, dimensions={0}, use_global_device_ids=true | all-gather | bytes 589824 | tf_op jit(solution)/shard_map/all_gather | solution.py:64
  42.8 0.9 constant_dynamic-slice_fusion.5
  43.7 33.2 %all_gather.20 = bf16[256,1024]{1,0:T(8,128)(2,1)} all-gather(bf16[32,1024]{1,0:T(8,128)(2,1)S(1)} %constant_dynamic-slice_fusion.5), channel_id=1, replica_groups=mesh['seq'=8,'samp'=4] {'seq'}, dimensions={0}, use_global_device_ids=true | all-gather | bytes 589824 | tf_op jit(solution)/shard_map/all_gather | solution.py:65
  76.9 0.7 all-gather.9.cloned.1.call-update
  77.7 0.5 all-gather.11.cloned.1.call-update
  78.3 0.8 copy.38
  79.1 1.4 copy.40
  81.2 19.7 %all-gather.7.cloned.1.call-done = bf16[1024,1024]{1,0:T(8,128)(2,1)} async-done(((bf16[256,1024]{1,0:T(8,128)(2,1)}), bf16[1024,1024]{1,0:T(8,128)(2,1)}) %all-gather.7.cloned.1.call-update) | async-done | bytes 2097168 | tf_op jit(solution)/shard_map/all_gather | solution.py:69
  100.9 45.4 %while.35 = (s32[]{:T(128)}, f32[1,8,5,128]{3,2,1,0:T(8,128)S(1)}, f32[1,8,5,128]{3,2,1,0:T(8,128)}, f32[1,128,8,5,128]{1,4,3,2,0:T(8,128)}, s32[2,512]{1,0:T(2,...) while((s32[]{:T(128)}, f32[1,8,5,128]{3,2,1,0:T(8,128)S(1)}, ...), condition=%wide.region_4.5_spmd.clone, body=%wide.region_0.4_spmd.clone.sunk | while | flops 1373029888 | bytes 80294112 | solution.py:95
  101.0 1.7 constant_dynamic-slice_fusion.11
  102.7 0.5 copy.66
  103.3 6.7 %fusion.66 = (f32[8,5,128]{2,1,0:T(8,128)S(1)}, f32[8,512,128,5]{2,1,3,0:T(8,128)}) fusion(pred[512]{0:T(512)(128)(4,1)S(1)} %broadcast_compare_fusion.5, bf16[512,8,128,1]{0,2,3,1:T(8,128)(2,1)S(1)} %bitcast.194, bf16[1,128,8,5,128]{4,1,3,2,0:T(8,128)(2,1)} %get-tuple-element.613), kind=kOutput, calls=%fused_computation.3.clone.1 | convolution fusion | flops 678947840 | bytes 12866048 | tf_op jit(solution)/shard_map/while/body/eval_jaxpr/sqgjd,rgd->sgjqr/dot_general | solution.py:87
  110.0 1.4 copy.67
  111.4 8.5 %bitcast_add_fusion.11 = f32[1,128,8,5,128]{1,4,3,2,0:T(8,128)} fusion(f32[1,128,8,5,128]{1,4,3,2,0:T(8,128)} %get-tuple-element.598, bf16[512,8,128,1]{0,2,3,1:T(8,128)(2,1)} %bitcast.197, f32[8,512,128,5]{2,1,3,0:T(8,128)} %get-tuple-element.581, f32[8,5,128]{2,1,0:T(8,128)S(1)} %bitcast.200, pred[512]{0:T(512)(128)(4,1)S(1)} %broadcast_compare_fusion.5, ...), kind=kOutput, calls=%fused_computation.14.clone.1 | convolution fusion | flops 683540480 | bytes 16818688 | tf_op jit(solution)/shard_map/while/body/eval_jaxpr/sgjqr,rgd->sqgjd/dot_general | solution.py:30
  119.8 2.3 fusion.68
  122.1 0.6 bitcast_add_fusion.10
  122.9 1.7 constant_dynamic-slice_fusion.11
  124.6 0.5 copy.66
  125.2 6.8 %fusion.66 = (f32[8,5,128]{2,1,0:T(8,128)S(1)}, f32[8,512,128,5]{2,1,3,0:T(8,128)}) fusion(pred[512]{0:T(512)(128)(4,1)S(1)} %broadcast_compare_fusion.5, bf16[512,8,128,1]{0,2,3,1:T(8,128)(2,1)S(1)} %bitcast.194, bf16[1,128,8,5,128]{4,1,3,2,0:T(8,128)(2,1)} %get-tuple-element.613), kind=kOutput, calls=%fused_computation.3.clone.1 | convolution fusion | flops 678947840 | bytes 12866048 | tf_op jit(solution)/shard_map/while/body/eval_jaxpr/sqgjd,rgd->sgjqr/dot_general | solution.py:87
  132.0 1.4 copy.67
  133.3 9.2 %bitcast_add_fusion.11 = f32[1,128,8,5,128]{1,4,3,2,0:T(8,128)} fusion(f32[1,128,8,5,128]{1,4,3,2,0:T(8,128)} %get-tuple-element.598, bf16[512,8,128,1]{0,2,3,1:T(8,128)(2,1)} %bitcast.197, f32[8,512,128,5]{2,1,3,0:T(8,128)} %get-tuple-element.581, f32[8,5,128]{2,1,0:T(8,128)S(1)} %bitcast.200, pred[512]{0:T(512)(128)(4,1)S(1)} %broadcast_compare_fusion.5, ...), kind=kOutput, calls=%fused_computation.14.clone.1 | convolution fusion | flops 683540480 | bytes 16818688 | tf_op jit(solution)/shard_map/while/body/eval_jaxpr/sgjqr,rgd->sqgjd/dot_general | solution.py:30
  142.6 2.3 fusion.68
  144.9 1.4 bitcast_add_fusion.10
  146.3 5.9 %all-gather.9.cloned.1.call-done = bf16[1,1024,1024]{2,1,0:T(8,128)(2,1)} async-done(((bf16[1,128,1024]{2,1,0:T(8,128)(2,1)}), bf16[1,1024,1024]{2,1,0:T(8,128)(2,1)}) %all-gather.9.cloned.1.call-update) | async-done | bytes 2097168 | tf_op jit(solution)/shard_map/all_gather | solution.py:105
  152.2 49.6 %all-gather.11.cloned.1.call-done = bf16[1,1024,1024]{2,1,0:T(8,128)(2,1)} async-done(((bf16[1,128,1024]{2,1,0:T(8,128)(2,1)}), bf16[1,1024,1024]{2,1,0:T(8,128)(2,1)}) %all-gather.11.cloned.1.call-update) | async-done | bytes 2097168 | tf_op jit(solution)/shard_map/all_gather | solution.py:106
  201.8 50.6 %while.34 = (s32[]{:T(128)}, f32[1,8,5,128]{3,2,1,0:T(8,128)S(1)}, f32[1,8,5,128]{3,2,1,0:T(8,128)}, f32[1,128,8,5,128]{1,4,3,2,0:T(8,128)}, s32[2,512]{1,0:T(2,...) while((s32[]{:T(128)}, f32[1,8,5,128]{3,2,1,0:T(8,128)S(1)}, ...), condition=%wide.region_9.10_spmd.clone, body=%wide.region_5.9_spmd.clone.sunk | while | flops 1372491392 | bytes 80563432 | solution.py:131
  201.8 0.7 select_reduce_fusion.4
  202.6 0.2 compare_and_fusion.2
  202.8 1.7 constant_dynamic-slice_fusion.10
  204.5 0.5 copy.64
  205.1 7.2 %fusion.60 = (f32[8,5,128]{2,1,0:T(8,128)S(1)}, f32[8,512,128,5]{2,1,3,0:T(8,128)}) fusion(pred[128,512]{0,1:T(8,128)(4,1)S(1)} %compare_and_fusion.2, bf16[512,8,128,1]{0,2,3,1:T(8,128)(2,1)S(1)} %bitcast.195, bf16[1,128,8,5,128]{4,1,3,2,0:T(8,128)(2,1)} %get-tuple-element.649), kind=kOutput, calls=%fused_computation.36.clone.1 | convolution fusion | flops 678947840 | bytes 12931072 | tf_op jit(solution)/shard_map/while/body/eval_jaxpr/sqgjd,srgd->sgjqr/dot_general | solution.py:118
  212.3 0.6 fusion.61
  212.9 1.4 copy.65
  214.3 9.1 %bitcast_add_fusion.9 = f32[1,128,8,5,128]{1,4,3,2,0:T(8,128)} fusion(f32[1,128,8,5,128]{1,4,3,2,0:T(8,128)} %get-tuple-element.632, bf16[512,8,128,1]{0,2,3,1:T(8,128)(2,1)} %bitcast.196, f32[8,512,128,5]{2,1,3,0:T(8,128)} %get-tuple-element.566, f32[8,5,128]{2,1,0:T(8,128)S(1)} %bitcast.198, pred[128,512]{0,1:T(8,128)(4,1)S(1)} %compare_and_fusion.2, ...), kind=kOutput, calls=%fused_computation.47.clone.1 | convolution fusion | flops 682885120 | bytes 16883712 | tf_op jit(solution)/shard_map/while/body/eval_jaxpr/sgjqr,srgd->sqgjd/dot_general | solution.py:30
  223.5 2.3 fusion.62
  225.7 1.4 bitcast_add_fusion.8
  227.1 0.7 select_reduce_fusion.4
  228.1 1.7 constant_dynamic-slice_fusion.10
  229.9 0.5 copy.64
  230.4 7.2 %fusion.60 = (f32[8,5,128]{2,1,0:T(8,128)S(1)}, f32[8,512,128,5]{2,1,3,0:T(8,128)}) fusion(pred[128,512]{0,1:T(8,128)(4,1)S(1)} %compare_and_fusion.2, bf16[512,8,128,1]{0,2,3,1:T(8,128)(2,1)S(1)} %bitcast.195, bf16[1,128,8,5,128]{4,1,3,2,0:T(8,128)(2,1)} %get-tuple-element.649), kind=kOutput, calls=%fused_computation.36.clone.1 | convolution fusion | flops 678947840 | bytes 12931072 | tf_op jit(solution)/shard_map/while/body/eval_jaxpr/sqgjd,srgd->sgjqr/dot_general | solution.py:118
  237.6 0.6 fusion.61
  238.3 1.4 copy.65
  239.6 9.1 %bitcast_add_fusion.9 = f32[1,128,8,5,128]{1,4,3,2,0:T(8,128)} fusion(f32[1,128,8,5,128]{1,4,3,2,0:T(8,128)} %get-tuple-element.632, bf16[512,8,128,1]{0,2,3,1:T(8,128)(2,1)} %bitcast.196, f32[8,512,128,5]{2,1,3,0:T(8,128)} %get-tuple-element.566, f32[8,5,128]{2,1,0:T(8,128)S(1)} %bitcast.198, pred[128,512]{0,1:T(8,128)(4,1)S(1)} %compare_and_fusion.2, ...), kind=kOutput, calls=%fused_computation.47.clone.1 | convolution fusion | flops 682885120 | bytes 16883712 | tf_op jit(solution)/shard_map/while/body/eval_jaxpr/sgjqr,srgd->sqgjd/dot_general | solution.py:30
  248.8 2.3 fusion.62
  251.0 1.4 bitcast_add_fusion.8
  252.4 2.1 select_convert_fusion
  254.6 1.4 copy.45
  (67 shorter events, 0.9 us)
Async XLA Ops:
  6.5 1.0 copy-start
  6.5 71.8 %copy-start.1 = (bf16[1,128,5120]{2,1,0:T(8,128)(2,1)S(1)}, bf16[1,128,5120]{2,1,0:T(8,128)(2,1)}, u32[]{:S(2)}) copy-start(bf16[1,128,5120]{2,1,0:T(8,128)(2,1)} %param.12) | copy-start | bytes 3932164
  6.5 74.7 %all-gather.5.cloned.1.call-start = ((), (), s32[]{:S(2)}) async-start(), calls=%async_computation | async-start | bytes 2621440 | tf_op jit(solution)/shard_map/all_gather | solution.py:68
  42.8 58.1 %all-gather.7.cloned.1.call-start = ((), (), s32[]{:S(2)}) async-start(), calls=%async_computation.1 | async-start | bytes 2621440 | tf_op jit(solution)/shard_map/all_gather | solution.py:69
  76.9 75.3 %all-gather.9.cloned.1.call-start = ((), (), s32[]{:S(2)}) async-start(), calls=%async_computation.2 | async-start | bytes 2359296 | tf_op jit(solution)/shard_map/all_gather | solution.py:105
  77.6 124.2 %all-gather.11.cloned.1.call-start = ((), (), s32[]{:S(2)}) async-start(), calls=%async_computation.3 | async-start | bytes 2359296 | tf_op jit(solution)/shard_map/all_gather | solution.py:106
  78.3 22.6 %copy-start.2 = (s32[1,1,8]{2,1,0:T(1,128)S(1)}, s32[1,1,8]{2,1,0:T(1,128)}, u32[]{:S(2)}) copy-start(s32[1,1,8]{2,1,0:T(1,128)} %param.17) | copy-start | bytes 100
  110.0 9.8 %slice-start.3 = ((s8[10485760]{0:T(1024)(128)(4,1)}), s8[2097152]{0:T(1024)(128)(4,1)S(1)}, s32[]{:S(2)}) async-start(s8[10485760]{0:T(1024)(128)(4,1)} %bitcast.192), calls=%async_computation.7 | async-start | bytes 4194304 | tf_op jit(solution)/shard_map/while
  111.4 8.5 %slice-start.4 = ((s8[10485760]{0:T(1024)(128)(4,1)}), s8[4194304]{0:T(1024)(128)(4,1)S(1)}, s32[]{:S(2)}) async-start(s8[10485760]{0:T(1024)(128)(4,1)} %bitcast.192), calls=%async_computation.8 | async-start | bytes 8388608 | tf_op jit(solution)/shard_map/while
  111.4 8.5 %slice-start.5 = ((s8[10485760]{0:T(1024)(128)(4,1)}), s8[4194304]{0:T(1024)(128)(4,1)S(1)}, s32[]{:S(2)}) async-start(s8[10485760]{0:T(1024)(128)(4,1)} %bitcast.192), calls=%async_computation.9 | async-start | bytes 8388608 | tf_op jit(solution)/shard_map/while
  132.0 10.6 %slice-start.3 = ((s8[10485760]{0:T(1024)(128)(4,1)}), s8[2097152]{0:T(1024)(128)(4,1)S(1)}, s32[]{:S(2)}) async-start(s8[10485760]{0:T(1024)(128)(4,1)} %bitcast.192), calls=%async_computation.7 | async-start | bytes 4194304 | tf_op jit(solution)/shard_map/while
  133.3 9.2 %slice-start.4 = ((s8[10485760]{0:T(1024)(128)(4,1)}), s8[4194304]{0:T(1024)(128)(4,1)S(1)}, s32[]{:S(2)}) async-start(s8[10485760]{0:T(1024)(128)(4,1)} %bitcast.192), calls=%async_computation.8 | async-start | bytes 8388608 | tf_op jit(solution)/shard_map/while
  133.3 9.2 %slice-start.5 = ((s8[10485760]{0:T(1024)(128)(4,1)}), s8[4194304]{0:T(1024)(128)(4,1)S(1)}, s32[]{:S(2)}) async-start(s8[10485760]{0:T(1024)(128)(4,1)} %bitcast.192), calls=%async_computation.9 | async-start | bytes 8388608 | tf_op jit(solution)/shard_map/while
  212.9 10.5 %slice-start = ((s8[10485760]{0:T(1024)(128)(4,1)}), s8[2097152]{0:T(1024)(128)(4,1)S(1)}, s32[]{:S(2)}) async-start(s8[10485760]{0:T(1024)(128)(4,1)} %bitcast.190), calls=%async_computation.4 | async-start | bytes 4194304 | tf_op jit(solution)/shard_map/while
  214.3 9.1 %slice-start.1 = ((s8[10485760]{0:T(1024)(128)(4,1)}), s8[4194304]{0:T(1024)(128)(4,1)S(1)}, s32[]{:S(2)}) async-start(s8[10485760]{0:T(1024)(128)(4,1)} %bitcast.190), calls=%async_computation.5 | async-start | bytes 8388608 | tf_op jit(solution)/shard_map/while
  214.3 9.1 %slice-start.2 = ((s8[10485760]{0:T(1024)(128)(4,1)}), s8[4194304]{0:T(1024)(128)(4,1)S(1)}, s32[]{:S(2)}) async-start(s8[10485760]{0:T(1024)(128)(4,1)} %bitcast.190), calls=%async_computation.6 | async-start | bytes 8388608 | tf_op jit(solution)/shard_map/while
  238.3 10.5 %slice-start = ((s8[10485760]{0:T(1024)(128)(4,1)}), s8[2097152]{0:T(1024)(128)(4,1)S(1)}, s32[]{:S(2)}) async-start(s8[10485760]{0:T(1024)(128)(4,1)} %bitcast.190), calls=%async_computation.4 | async-start | bytes 4194304 | tf_op jit(solution)/shard_map/while
  239.6 9.1 %slice-start.1 = ((s8[10485760]{0:T(1024)(128)(4,1)}), s8[4194304]{0:T(1024)(128)(4,1)S(1)}, s32[]{:S(2)}) async-start(s8[10485760]{0:T(1024)(128)(4,1)} %bitcast.190), calls=%async_computation.5 | async-start | bytes 8388608 | tf_op jit(solution)/shard_map/while
  239.6 9.1 %slice-start.2 = ((s8[10485760]{0:T(1024)(128)(4,1)}), s8[4194304]{0:T(1024)(128)(4,1)S(1)}, s32[]{:S(2)}) async-start(s8[10485760]{0:T(1024)(128)(4,1)} %bitcast.190), calls=%async_computation.6 | async-start | bytes 8388608 | tf_op jit(solution)/shard_map/while
Sparse Core Ops, SparseCore 0:
  42.9 23.6 all-gather.4
  77.0 23.8 all-gather.6
  103.0 49.0 all-gather.8
  154.2 47.5 all-gather.10
where the time goes:
time: 263 us
  waiting for transfers between devices  76.5 us (29%)
  blocking collectives  68.5 us (26%)
  matrix products  63.9 us (24%)
  local copies, waits for them, and re-layouts  20 us (8%)
  other arithmetic  19.6 us (7%)
  between operations  13.9 us (5%)
    all_gather x1, waiting for transfers between devices, shards(): value_rows = lax.all_gather(suffix_values, 'seq', axis=1, tiled=True)  49.6 us
    dot_general x4, matrix products, softmax_step(): jnp.einsum(form, rounded, value_rows, preferred_element_type=jnp.float32)  35.9 us
    all_gather x1, blocking collectives, shards(): lax.all_gather(own_keys, 'seq', axis=0, tiled=True)  35.3 us
    all_gather x1, blocking collectives, shards(): lax.all_gather(own_values, 'seq', axis=0, tiled=True)  33.2 us
    all_gather x1, waiting for transfers between devices, shards(): lax.all_gather(shares[1], 'samp', axis=0, tiled=True)  19.7 us
    dot_general x2, matrix products, suffix_one_step(): jnp.einsum('sqgjd,srgd->sgjqr', query_grid, key_grid, preferred_element_t...  14.5 us
    dot_general x2, matrix products, prefix_one_step(): jnp.einsum('sqgjd,rgd->sgjqr', query_grid, key_grid, preferred_element_ty...  13.5 us
    reduce_sum x4, other arithmetic, softmax_step(): new_sum = run_sum * scale_old + jnp.sum(weights, axis=-1)  9.15 us
  transfers between devices with their start and end apart: 4, of which 3 were waited for; matrix products, arithmetic and copies ran while one was open for 18% of the time, Pallas kernels for 0%

commit v1 on v0

v1 whole, which is shorter than its diff:
```python
import functools
import math

import jax
import jax.numpy as jnp
from jax import lax
from jax.experimental import pallas as pl
from jax.experimental.pallas import tpu as pltpu
from jax.sharding import PartitionSpec as P


HEADS = 40
KV_HEADS = 8
HEAD_DIM = 128
BLOCK = 128
GROUP = HEADS // KV_HEADS
WIDE = GROUP * BLOCK
COLUMNS = 2
TOGETHER = 2
CHUNK = 4


masked_value = -1e30
exponent_scale = math.log2(math.e) / math.sqrt(HEAD_DIM)


def pack_kernel(heads, first_ref, key_ref, value_ref, out_ref):
    for n in range(heads):
        lanes = pl.ds(pl.multiple_of((first_ref[0] + n) * HEAD_DIM, HEAD_DIM), HEAD_DIM)
        out_ref[n, 0] = key_ref[:, lanes]
        out_ref[n, 1] = value_ref[:, lanes].T


def pack(keys, values, first_head, heads):
    inside = pl.BlockSpec(memory_space=pltpu.VMEM)
    return pl.pallas_call(
        functools.partial(pack_kernel, heads),
        out_shape=pltpu.VMEM((heads, 2, BLOCK, HEAD_DIM), keys.dtype),
        in_specs=[pl.BlockSpec(memory_space=pltpu.SMEM), inside, inside],
        out_specs=inside,
        compiler_params=pltpu.CompilerParams(vmem_limit_bytes=4 * 2**20),
        name="pack",
    )(
        first_head,
        pltpu.with_memory_space_constraint(keys, pltpu.VMEM),
        pltpu.with_memory_space_constraint(values, pltpu.VMEM),
    )


def head_of(step, samp_index, shares):
    per_share = KV_HEADS // shares
    half = KV_HEADS // 2
    core_rel = step // half
    inner = step % half
    x_rel = inner // per_share
    share = samp_index ^ (x_rel * 2 + core_rel)
    return share * per_share + inner % per_share


def attend_kernel(plan, place, pre_row, suf_row, lengths, query_ref, *refs):
    slots, prefix_count, rows, shares, first, last = plan
    refs = list(refs)
    block_refs = [[refs.pop(0) for _ in range(parts)] for slot, parts in slots]
    slots = [slot for slot, parts in slots]
    prefix_refs = [refs.pop(0) for _ in range(8)] if prefix_count else []
    state_ref = None if first else refs.pop(0)
    out_ref = refs.pop(0)
    if first or not last:
        state_ref = out_ref
    key_buffer, value_buffer, seen_list = refs
    half = KV_HEADS // 2
    per_share = KV_HEADS // shares
    seq_index, samp_index = place[0], place[1]
    row, column = seq_index // COLUMNS, seq_index % COLUMNS
    live = seq_index < lengths[0]

    def suffix_seen(slot):
        back, across = slot
        side = 1 - column if across else column
        block = (row - back) * COLUMNS + side
        inside = (block >= 0) & (block < seq_index)
        return inside & (suf_row[jnp.maximum(block, 0)] > 0)

    def prefix_seen(n):
        side = jnp.where(n >= rows, 1 - column, column)
        back = n % rows
        block = jnp.where(row >= back, row - back, row - back + rows) * COLUMNS + side
        return pre_row[block] > 0

    @pl.when(live)
    def compute():
        places, suffix_end = [], jnp.int32(0)
        for slot in slots:
            seen = True if slot == (0, False) else suffix_seen(slot)
            places.append((seen, suffix_end))
            suffix_end = suffix_end + (1 if seen is True else seen.astype(jnp.int32))
        near_count = prefix_seen_count = jnp.int32(0)
        if prefix_count:

            def note(n, found):
                seen_list[found] = n
                return found + prefix_seen(n).astype(jnp.int32)

            near_count = lax.fori_loop(0, rows, note, jnp.int32(0))
            prefix_seen_count = lax.fori_loop(rows, prefix_count, note, near_count)
        count = suffix_end + prefix_seen_count

        def some_heads(turn, unused):
            step = turn * TOGETHER
            head = head_of(step, samp_index, shares)
            inner = step % half
            lanes = range(TOGETHER)

            def take(position, sources):
                for i, source in enumerate(sources):
                    key_buffer[i, position] = source[0]
                    value_buffer[i, position] = source[1]

            def take_block(n, position):
                parts = block_refs[n]
                height = KV_HEADS // len(parts)
                for m, part in enumerate(parts):

                    @pl.when((head >= m * height) & (head < (m + 1) * height))
                    def _(m=m, part=part):
                        take(position, [part.at[head - m * height + i] for i in lanes])

            for n, (seen, position) in enumerate(places):
                if seen is True:
                    take_block(n, position)
                else:
                    pl.when(seen)(functools.partial(take_block, n, position))

            for way in range(4 if prefix_count else 0):
                pieces = prefix_refs[way * 2 : way * 2 + 2]

                def take_prefix(ref, skipped, n, unused):
                    chosen = ref.at[seen_list[n] - skipped]
                    first_head = inner % per_share
                    take(suffix_end + n, [chosen.at[first_head + i] for i in lanes])
                    return unused

                @pl.when(step // per_share == way)
                def _(pieces=pieces):
                    lax.fori_loop(0, near_count, functools.partial(take_prefix, pieces[0], 0), 0)
                    lax.fori_loop(
                        near_count,
                        prefix_seen_count,
                        functools.partial(take_prefix, pieces[1], rows),
                        0,
                    )

            offset = pl.multiple_of(head * WIDE, WIDE)
            wide = query_ref[:, pl.ds(offset, TOGETHER * WIDE)]
            queries = [
                jnp.concatenate(
                    [
                        wide[:, (i * GROUP + j) * HEAD_DIM : (i * GROUP + j + 1) * HEAD_DIM]
                        for j in range(GROUP)
                    ],
                    axis=0,
                )
                for i in lanes
            ]
            state = [state_ref.at[step + i] for i in lanes]
            sums = slice(HEAD_DIM + 8, HEAD_DIM + 16)

            def chunk(start, size, fresh):
                keys = [
                    key_buffer[i, pl.ds(start, size)].reshape(size * BLOCK, HEAD_DIM)
                    for i in lanes
                ]
                values = [
                    jnp.concatenate([value_buffer[i, start + n] for n in range(size)], axis=1)
                    for i in lanes
                ]
                before = [None if fresh else state[i][HEAD_DIM:] for i in lanes]
                tall = size * BLOCK // 8
                after = []
                for i in lanes:
                    scores = lax.dot_general(
                        keys[i],
                        queries[i],
                        (((1,), (1,)), ((), ())),
                        preferred_element_type=jnp.float32,
                    )
                    if fresh:
                        key_at = lax.broadcasted_iota(jnp.int32, (BLOCK, WIDE), 0)
                        query_at = lax.broadcasted_iota(jnp.int32, (BLOCK, WIDE), 1) % BLOCK
                        scores = jnp.where(key_at <= query_at, scores, masked_value)
                    new = jnp.max(scores, axis=0, keepdims=True)
                    if not fresh:
                        new = jnp.maximum(before[i][0:1], new)
                    weights = jnp.exp2((scores - new) * exponent_scale)
                    part_sum = jnp.sum(weights.reshape(tall, 8, WIDE), axis=0)
                    part = lax.dot_general(
                        values[i],
                        weights.astype(jnp.bfloat16),
                        (((1,), (0,)), ((), ())),
                        preferred_element_type=jnp.float32,
                    )
                    after.append((new, part_sum, part))
                for i in lanes:
                    new, part_sum, part = after[i]
                    if not fresh:
                        shrink = jnp.exp2((before[i][0:1] - new) * exponent_scale)
                        part_sum = part_sum + before[i][8:] * shrink
                        part = part + state[i][:HEAD_DIM] * shrink
                    state[i][:HEAD_DIM] = part
                    state[i][HEAD_DIM : HEAD_DIM + 8] = jnp.broadcast_to(new, (8, WIDE))
                    state[i][sums] = part_sum

            start = 0
            if first:
                chunk(0, 1, True)
                start = 1
            rest = count - start

            def many(n, unused):
                chunk(start + n * CHUNK, CHUNK, False)
                return unused

            largest = len(slots) + prefix_count - start
            if largest >= CHUNK:
                lax.fori_loop(0, rest // CHUNK, many, 0)
            size = CHUNK // 2
            while size:
                if largest >= size:

                    @pl.when(rest // size % 2 == 1)
                    def _(size=size):
                        chunk(start + rest // (2 * size) * (2 * size), size, False)

                size //= 2

            if last:
                parts = []
                for i in lanes:
                    inverse = 1.0 / jnp.sum(state[i][sums], axis=0, keepdims=True)
                    mixed = (state[i][:HEAD_DIM] * inverse).astype(jnp.bfloat16)
                    parts += [mixed[:, j * BLOCK : (j + 1) * BLOCK].T for j in range(GROUP)]
                out_ref[:, pl.ds(offset, TOGETHER * WIDE)] = jnp.concatenate(parts, axis=1)
            return unused

        lax.fori_loop(0, KV_HEADS // TOGETHER, some_heads, 0)

    if last:

        @pl.when(jnp.logical_not(live))
        def blank():
            out_ref[...] = jnp.zeros_like(out_ref)


def attend(tables, queries, slots, blocks, prefix, state, shares, rows, last):
    prefix_count = prefix[0].shape[0] * COLUMNS if prefix else 0
    first = state is None
    total = len(slots) + prefix_count
    plan = tuple((slot, len(parts)) for slot, parts in zip(slots, blocks))
    blocks = [part for parts in blocks for part in parts]
    state_shape = (KV_HEADS, HEAD_DIM + 16, WIDE)
    if last:
        out_shape = jax.ShapeDtypeStruct((BLOCK, HEADS * HEAD_DIM), jnp.bfloat16)
    else:
        out_shape = pltpu.VMEM(state_shape, jnp.float32)
    operands = [queries, *blocks, *prefix] + ([] if first else [state])
    operands = [pltpu.with_memory_space_constraint(x, pltpu.VMEM) for x in operands]
    inside = pl.BlockSpec(memory_space=pltpu.VMEM)
    table = pl.BlockSpec(memory_space=pltpu.SMEM)
    aliases = {} if first or last else {len(tables) + len(operands) - 1: 0}
    return pl.pallas_call(
        functools.partial(
            attend_kernel, (plan, prefix_count, rows, shares, first, last)
        ),
        out_shape=out_shape,
        in_specs=[table] * len(tables) + [inside] * len(operands),
        out_specs=inside,
        scratch_shapes=[
            pltpu.VMEM((TOGETHER, total, BLOCK, HEAD_DIM), jnp.bfloat16),
            pltpu.VMEM((TOGETHER, total, HEAD_DIM, BLOCK), jnp.bfloat16),
            pltpu.SMEM((max(prefix_count, 1) + 1,), jnp.int32),
        ],
        input_output_aliases=aliases,
        compiler_params=pltpu.CompilerParams(vmem_limit_bytes=10 * 2**20 + total * 2**17),
    )(*tables, *operands)


def shards(
    queries, prefix_keys, prefix_values, suffix_keys, suffix_values, layout_pre, layout_suf, lengths
):
    seq_count = lax.axis_size("seq")
    shares = lax.axis_size("samp")
    rows = seq_count // COLUMNS
    seq_index = lax.axis_index("seq")
    samp_index = lax.axis_index("samp")
    per_share = KV_HEADS // shares

    def along_rows(pairs):
        return [(a * COLUMNS + y, b * COLUMNS + y) for a, b in pairs for y in range(COLUMNS)]

    def move(value, pairs, axis="seq"):
        return lax.ppermute(value, axis, pairs)

    swap_columns = [(i, i ^ 1) for i in range(seq_count)]
    own = pack(suffix_keys[0], suffix_values[0], jnp.zeros(1, jnp.int32), KV_HEADS)
    first_head = (samp_index * per_share).astype(jnp.int32)
    own_share = pack(prefix_keys, prefix_values, first_head[None], per_share)

    held = {(0, False): own}
    across = [(z * COLUMNS, z * COLUMNS + 1) for z in range(rows)]
    held[0, True] = move(own, across)
    for k in range(1, rows):
        upward = along_rows([(z, z + 1) for z in range(k - 1, rows - 1)])
        held[k, False] = move(held[k - 1, False], upward)
        if k < rows - 1:
            held[k, True] = move(held[k, False], swap_columns[k * COLUMNS :])
    low = slice(0, KV_HEADS // 2)
    high = slice(KV_HEADS // 2, KV_HEADS)
    top = rows - 1
    from_side = move(held[top, False][low], swap_columns[top * COLUMNS :])
    source = held[top - 1, True] if top > 1 else move(own, [(1, 0)] + across[:1])
    from_below = move(source[high], along_rows([(top - 1, top)]))
    held[top, True] = (from_side, from_below)

    gathered = [own_share]
    for k in range(1, rows):
        turn = along_rows([(z, (z + k) % rows) for z in range(rows)])
        gathered.append(move(own_share, turn))
    swap_x = [(i, i ^ 2) for i in range(shares)]
    swap_core = [(i, i ^ 1) for i in range(shares)]
    same = jnp.stack(gathered)
    other = move(same, swap_columns)
    same_x = move(same, swap_x, "samp")
    other_x = move(other, swap_x, "samp")
    near = [same, other, same_x, other_x]
    far = [move(piece, swap_core, "samp") for piece in near]

    early, late = stages(rows)
    middle = [slot for slot in held if slot not in early and slot not in late]
    tables = (
        jnp.stack([seq_index, samp_index]).astype(jnp.int32),
        layout_pre[0, 0],
        layout_suf[0, 0],
        lengths,
    )

    def run(slots, prefix, state, last):
        blocks = [held[slot] if isinstance(held[slot], tuple) else (held[slot],) for slot in slots]
        return attend(tables, queries[0], slots, blocks, prefix, state, shares, rows, last)

    state = run(early, [], None, False)
    state = run(middle, near + far, state, False)
    return run(late, [], state, True)[None]


def stages(rows):
    early = [(0, False), (0, True)] + [(1, False)] * (rows > 2)
    late = [(rows - 1, False), (rows - 1, True)]
    if rows > 2:
        late.insert(0, (rows - 2, True))
    return early, [slot for slot in late if slot not in early]


def solution(mesh):
    return jax.shard_map(
        shards,
        mesh=mesh,
        in_specs=(
            P("samp", "seq", None),
            P("seq", None),
            P("seq", None),
            P("samp", "seq", None),
            P("samp", "seq", None),
            P("samp", "seq", None),
            P("samp", "seq", None),
            P("samp"),
        ),
        out_specs=P("samp", "seq", None),
        check_vma=False,
    )
```

time: 263 us -> 104 us (0.40)
  the two profiles are of different devices: /device:TPU:0 before, /device:TPU:26 now
where the time goes in v1:
time: 104 us; the launch traced here: 103 us
  waiting for transfers between devices  38.1 us (37%)
  starting transfers between devices  28.5 us (27%)
  Pallas kernels  23.6 us (23%)
  local copies, waits for them, and re-layouts  12 us (12%)
    ppermute x18, waiting for transfers between devices, move(): return lax.ppermute(value, axis, pairs)  38.1 us
    ppermute x18, starting transfers between devices, move(): return lax.ppermute(value, axis, pairs)  28.5 us
    pallas_call x3, Pallas kernels, attend(): pl.pallas_call(functools.partial(attend_kernel, (plan, prefix_count, rows...  23.3 us
    unnamed x38, local copies, waits for them, and re-layouts  10.5 us
  transfers between devices with their start and end apart: 18, of which 6 were waited for; matrix products, arithmetic and copies ran while one was open for 2% of the time, Pallas kernels for 18%

profile of v1, /device:TPU:26, one launch (start us, length us, event | category | flops | bytes accessed | tf_op | source)
XLA Modules:
  0.0 103.4 jit_solution(4779493748381084718)
XLA Ops:
  0.0 1.1 %copy-done.13 = bf16[1,128,1024]{2,1,0:T(8,128)(2,1)S(1)} copy-done((bf16[1,128,1024]{2,1,0:T(8,128)(2,1)S(1)}, bf16[1,128,1024]{2,1,0:T(8,128)(2,1)}, u32[]{:S(2)}) %copy-start.13) | copy-done | bytes 262168
  1.1 0.9 copy-done.14
  2.0 0.2 pack.2.refs_0_
  2.2 1.3 %collective-permute-start = (bf16[8,2,128,128]{3,2,1,0:T(8,128)(2,1)S(1)}, bf16[8,2,128,128]{3,2,1,0:T(8,128)(2,1)S(1)}, u32[]{:S(2)}, u32[]{:S(2)}) collective-permute-start(bf16[8,2,128,128]{3,2,1,0:T(8,128)(2,1)S(1)} %pack.2.refs_0_), channel_id=1, source_target_pairs={{0,8},{4,12},{8,16},{12,20},{16,24},{20,28},{1,9},{5,13},{9,17},{1... | collective-permute-start | bytes 1572872 | tf_op jit(solution)/shard_map/ppermute | solution.py:301
  3.5 0.0 copy-start.11
  3.5 0.9 copy-done.11
  4.5 0.9 copy-done.12
  5.4 0.1 pack.3
  5.5 2.6 %collective-permute-start.8 = (bf16[2,2,128,128]{3,2,1,0:T(8,128)(2,1)S(1)}, bf16[2,2,128,128]{3,2,1,0:T(8,128)(2,1)S(1)}, u32[]{:S(2)}, u32[]{:S(2)}) collective-permute-start(bf16[2,2,128,128]{3,2,1,0:T(8,128)(2,1)S(1)} %pack.3), channel_id=1, source_target_pairs={{0,16},{4,20},{8,24},{12,28},{16,0},{20,4},{24,8},{28,12},{1,17},{... | collective-permute-start | bytes 393224 | tf_op jit(solution)/shard_map/ppermute | solution.py:301
  8.1 0.5 collective-permute-start.9
  8.6 3.3 %collective-permute-start.7 = (bf16[2,2,128,128]{3,2,1,0:T(8,128)(2,1)S(1)}, bf16[2,2,128,128]{3,2,1,0:T(8,128)(2,1)S(1)}, u32[]{:S(2)}, u32[]{:S(2)}) collective-permute-start(bf16[2,2,128,128]{3,2,1,0:T(8,128)(2,1)S(1)} %pack.3), channel_id=1, source_target_pairs={{0,8},{4,12},{8,16},{12,20},{16,24},{20,28},{24,0},{28,4},{1,9},{5... | collective-permute-start | bytes 393224 | tf_op jit(solution)/shard_map/ppermute | solution.py:301
  11.9 15.3 %collective-permute-done.8 = bf16[2,2,128,128]{3,2,1,0:T(8,128)(2,1)S(1)} collective-permute-done((bf16[2,2,128,128]{3,2,1,0:T(8,128)(2,1)S(1)}, bf16[2,2,128,128]{3,2,1,0:T(8,128)(2,1)S(1)}, u32[]{:S(2)}, u32[]{:S(2)}) %collective-permute-start.8) | collective-permute-done | bytes 131104 | tf_op jit(solution)/shard_map/ppermute | solution.py:301
  27.2 0.1 pad_maximum_fusion.refs_2_
  27.3 1.6 %collective-permute-start.10 = (bf16[4,2,2,128,128]{4,3,2,1,0:T(8,128)(2,1)S(1)}, bf16[4,2,2,128,128]{4,3,2,1,0:T(8,128)(2,1)}, u32[]{:S(2)}, u32[]{:S(2)}) collective-permute-start(bf16[4,2,2,128,128]{4,3,2,1,0:T(8,128)(2,1)S(1)} %pad_maximum_fusion.refs_2_), channel_id=1, source_target_pairs={{0,4},{4,0},{8,12},{12,8},{16,20},{20,16},{24,28},{28,24},{1,5},{5... | collective-permute-start | bytes 1572872 | tf_op jit(solution)/shard_map/ppermute | solution.py:301
  28.9 1.3 %collective-permute-start.1 = (bf16[8,2,128,128]{3,2,1,0:T(8,128)(2,1)S(1)}, bf16[8,2,128,128]{3,2,1,0:T(8,128)(2,1)S(1)}, u32[]{:S(2)}, u32[]{:S(2)}) collective-permute-start(bf16[8,2,128,128]{3,2,1,0:T(8,128)(2,1)S(1)} %collective-permute-done.refs_2_), channel_id=1, source_target_pairs={{8,16},{12,20},{16,24},{20,28},{9,17},{13,21},{17,25},{21,29},{10,... | collective-permute-start | bytes 1572872 | tf_op jit(solution)/shard_map/ppermute | solution.py:301
  30.2 2.4 %collective-permute-start.17 = (bf16[8,2,128,128]{3,2,1,0:T(8,128)(2,1)S(1)}, bf16[8,2,128,128]{3,2,1,0:T(8,128)(2,1)S(1)}, u32[]{:S(2)}, u32[]{:S(2)}) collective-permute-start(bf16[8,2,128,128]{3,2,1,0:T(8,128)(2,1)S(1)} %pack.2.refs_0_), channel_id=1, source_target_pairs={{0,4},{8,12},{16,20},{24,28},{1,5},{9,13},{17,21},{25,29},{2,6},{1... | collective-permute-start | bytes 1572872 | tf_op jit(solution)/shard_map/ppermute | solution.py:301
  32.6 0.6 collective-permute-start.11
  33.2 8.0 %collective-permute-done.10.refs_3_ = bf16[4,2,2,128,128]{4,3,2,1,0:T(8,128)(2,1)} collective-permute-done((bf16[4,2,2,128,128]{4,3,2,1,0:T(8,128)(2,1)S(1)}, bf16[4,2,2,128,128]{4,3,2,1,0:T(8,128)(2,1)}, u32[]{:S(2)}, u32[]{:S(2)}) %collective-permute-start.10) | collective-permute-done | bytes 524320 | tf_op jit(solution)/shard_map/ppermute | solution.py:301
  41.2 0.5 collective-permute-start.12
  41.7 2.1 %collective-permute-done.1.refs_1_ = bf16[8,2,128,128]{3,2,1,0:T(8,128)(2,1)S(1)} collective-permute-done((bf16[8,2,128,128]{3,2,1,0:T(8,128)(2,1)S(1)}, bf16[8,2,128,128]{3,2,1,0:T(8,128)(2,1)S(1)}, u32[]{:S(2)}, u32[]{:S(2)}) %collective-permute-start.1) | collective-permute-done | bytes 524320 | tf_op jit(solution)/shard_map/ppermute | solution.py:301
  43.8 1.3 %collective-permute-start.3 = (bf16[8,2,128,128]{3,2,1,0:T(8,128)(2,1)S(1)}, bf16[8,2,128,128]{3,2,1,0:T(8,128)(2,1)S(1)}, u32[]{:S(2)}, u32[]{:S(2)}) collective-permute-start(bf16[8,2,128,128]{3,2,1,0:T(8,128)(2,1)S(1)} %collective-permute-done.1.refs_1_), channel_id=1, source_target_pairs={{16,24},{20,28},{17,25},{21,29},{18,26},{22,30},{19,27},{23,31}} | collective-permute-start | bytes 1572872 | tf_op jit(solution)/shard_map/ppermute | solution.py:301
  45.1 2.4 %collective-permute-start.2 = (bf16[8,2,128,128]{3,2,1,0:T(8,128)(2,1)S(1)}, bf16[8,2,128,128]{3,2,1,0:T(8,128)(2,1)S(1)}, u32[]{:S(2)}, u32[]{:S(2)}) collective-permute-start(bf16[8,2,128,128]{3,2,1,0:T(8,128)(2,1)S(1)} %collective-permute-done.1.refs_1_), channel_id=1, source_target_pairs={{16,20},{20,16},{24,28},{28,24},{17,21},{21,17},{25,29},{29,25},{1... | collective-permute-start | bytes 1572872 | tf_op jit(solution)/shard_map/ppermute | solution.py:301
  47.5 0.8 copy-done.1
  48.3 4.1 %collective-permute-done.17.refs_1_ = bf16[8,2,128,128]{3,2,1,0:T(8,128)(2,1)S(1)} collective-permute-done((bf16[8,2,128,128]{3,2,1,0:T(8,128)(2,1)S(1)}, bf16[8,2,128,128]{3,2,1,0:T(8,128)(2,1)S(1)}, u32[]{:S(2)}, u32[]{:S(2)}) %collective-permute-start.17) | collective-permute-done | bytes 524320 | tf_op jit(solution)/shard_map/ppermute | solution.py:301
  52.4 0.8 copy-done.9
  53.2 4.4 %collective-permute-start.6 = (bf16[8,2,128,128]{3,2,1,0:T(8,128)(2,1)}, bf16[8,2,128,128]{3,2,1,0:T(8,128)(2,1)S(1)}, u32[]{:S(2)}, u32[]{:S(2)}) collective-permute-start(bf16[8,2,128,128]{3,2,1,0:T(8,128)(2,1)} %copy-done.7), channel_id=1, source_target_pairs={{8,12},{12,8},{16,20},{20,16},{24,28},{28,24},{9,13},{13,9},{17,21... | collective-permute-start | bytes 1572872 | tf_op jit(solution)/shard_map/ppermute | solution.py:301
  57.6 0.3 collective-permute-start.14
  57.9 0.3 collective-permute-start.15
  58.2 4.4 %collective-permute-done.2.refs_0_ = bf16[8,2,128,128]{3,2,1,0:T(8,128)(2,1)S(1)} collective-permute-done((bf16[8,2,128,128]{3,2,1,0:T(8,128)(2,1)S(1)}, bf16[8,2,128,128]{3,2,1,0:T(8,128)(2,1)S(1)}, u32[]{:S(2)}, u32[]{:S(2)}) %collective-permute-start.2) | collective-permute-done | bytes 524320 | tf_op jit(solution)/shard_map/ppermute | solution.py:301
  62.6 0.0 collective-permute-start.16
  62.6 0.7 slice.8
  63.4 0.7 slice.9
  64.1 0.0 collective-permute-done.13.refs_6_
  64.1 0.8 copy-done.3
  64.9 4.4 %collective-permute-start.4 = (bf16[4,2,128,128]{3,2,1,0:T(8,128)(2,1)}, bf16[4,2,128,128]{3,2,1,0:T(8,128)(2,1)}, u32[]{:S(2)}, u32[]{:S(2)}) collective-permute-start(bf16[4,2,128,128]{3,2,1,0:T(8,128)(2,1)} %slice.8), channel_id=1, source_target_pairs={{24,28},{28,24},{25,29},{29,25},{26,30},{30,26},{27,31},{31,27}} | collective-permute-start | bytes 786440 | tf_op jit(solution)/shard_map/ppermute | solution.py:301
  69.3 4.3 %collective-permute-done.6.refs_0_ = bf16[8,2,128,128]{3,2,1,0:T(8,128)(2,1)S(1)} collective-permute-done((bf16[8,2,128,128]{3,2,1,0:T(8,128)(2,1)}, bf16[8,2,128,128]{3,2,1,0:T(8,128)(2,1)S(1)}, u32[]{:S(2)}, u32[]{:S(2)}) %collective-permute-start.6) | collective-permute-done | bytes 524320 | tf_op jit(solution)/shard_map/ppermute | solution.py:301
  73.6 0.8 copy-done.5
  74.4 1.3 %collective-permute-start.5 = (bf16[4,2,128,128]{3,2,1,0:T(8,128)(2,1)}, bf16[4,2,128,128]{3,2,1,0:T(8,128)(2,1)}, u32[]{:S(2)}, u32[]{:S(2)}) collective-permute-start(bf16[4,2,128,128]{3,2,1,0:T(8,128)(2,1)} %slice.9), channel_id=1, source_target_pairs={{16,24},{20,28},{17,25},{21,29},{18,26},{22,30},{19,27},{23,31}} | collective-permute-start | bytes 786440 | tf_op jit(solution)/shard_map/ppermute | solution.py:301
  76.4 0.1 pad_add_fusion.place
  76.5 1.0 %copy-done.8 = bf16[8,2,128,128]{3,2,1,0:T(8,128)(2,1)S(1)} copy-done((bf16[8,2,128,128]{3,2,1,0:T(8,128)(2,1)S(1)}, bf16[8,2,128,128]{3,2,1,0:T(8,128)(2,1)}, u32[]{:S(2)}) %copy-start.8) | copy-done | bytes 524312
  77.6 1.0 %copy-done.10 = bf16[8,2,128,128]{3,2,1,0:T(8,128)(2,1)S(1)} copy-done((bf16[8,2,128,128]{3,2,1,0:T(8,128)(2,1)S(1)}, bf16[8,2,128,128]{3,2,1,0:T(8,128)(2,1)}, u32[]{:S(2)}) %copy-start.10) | copy-done | bytes 524312
  78.6 0.7 copy-done.15
  79.3 0.7 copy-done.17
  79.9 5.7 %shard_map.82.refs_10_ = f32[8,144,640]{2,1,0:T(8,128)S(1)} custom-call(s32[2]{0:T(128)S(1)} %pad_add_fusion.place, s32[8]{0:T(128)S(1)} %bitcast.19, s32[8]{0:T(128)S(1)} %bitcast.22, s32[1]{0:T(128)S(6)} %copy.11.lengths, bf16[128,5120]{1,0:T(8,128)(2,1)S(1)} %bitcast.13, bf16[8,2,128,128]{3,2,1,0:T(8,128)(2,1)S(1)} %pack.2.refs_0_, ...), custom_call_target="tpu_custom_call" | custom-call | tf_op jit(solution)/shard_map/pallas_call | solution.py:270
  85.6 0.0 collective-permute-done.14.refs_7_
  85.6 0.0 collective-permute-done.16.refs_9_
  85.7 12.6 %shard_map.83.refs_4_ = f32[8,144,640]{2,1,0:T(8,128)S(1)} custom-call(s32[2]{0:T(128)S(1)} %pad_add_fusion.place, s32[8]{0:T(128)S(1)} %bitcast.20, s32[8]{0:T(128)S(1)} %bitcast.23, s32[1]{0:T(128)S(6)} %copy.11.lengths, bf16[128,5120]{1,0:T(8,128)(2,1)S(1)} %bitcast.14, bf16[8,2,128,128]{3,2,1,0:T(8,128)(2,1)S(1)} %copy-done.6, ...), custom_call_target="tpu_custom_call", output_to_operand_aliasing={{}: (15, {})} | custom-call | tf_op jit(solution)/shard_map/pallas_call | solution.py:270
  98.3 5.1 %shard_map.84 = bf16[128,5120]{1,0:T(8,128)(2,1)} custom-call(s32[2]{0:T(128)S(1)} %pad_add_fusion.place, s32[8]{0:T(128)S(1)} %bitcast.21, s32[8]{0:T(128)S(1)} %bitcast.24, s32[1]{0:T(128)S(6)} %copy.11.lengths, bf16[128,5120]{1,0:T(8,128)(2,1)S(1)} %bitcast.15, bf16[8,2,128,128]{3,2,1,0:T(8,128)(2,1)S(1)} %collective-permute-done.2.refs_0_, ...), custom_call_target="tpu_custom_call" | custom-call | tf_op jit(solution)/shard_map/pallas_call | solution.py:270
  (35 shorter events, 0.1 us)
Async XLA Ops:
  0.0 76.5 %copy-start = (bf16[1,128,5120]{2,1,0:T(8,128)(2,1)S(1)}, bf16[1,128,5120]{2,1,0:T(8,128)(2,1)}, u32[]{:S(2)}) copy-start(bf16[1,128,5120]{2,1,0:T(8,128)(2,1)} %param.8) | copy-start | bytes 3932164
  0.0 1.1 %copy-start.13 = (bf16[1,128,1024]{2,1,0:T(8,128)(2,1)S(1)}, bf16[1,128,1024]{2,1,0:T(8,128)(2,1)}, u32[]{:S(2)}) copy-start(bf16[1,128,1024]{2,1,0:T(8,128)(2,1)} %param.11) | copy-start | bytes 786436
  1.1 0.9 copy-start.14
  2.2 26.7 %collective-permute-start = (bf16[8,2,128,128]{3,2,1,0:T(8,128)(2,1)S(1)}, bf16[8,2,128,128]{3,2,1,0:T(8,128)(2,1)S(1)}, u32[]{:S(2)}, u32[]{:S(2)}) collective-permute-start(bf16[8,2,128,128]{3,2,1,0:T(8,128)(2,1)S(1)} %pack.2.refs_0_), channel_id=1, source_target_pairs={{0,8},{4,12},{8,16},{12,20},{16,24},{20,28},{1,9},{5,13},{9,17},{1... | collective-permute-start | bytes 1572872 | tf_op jit(solution)/shard_map/ppermute | solution.py:301
  3.5 1.0 copy-start.11
  4.5 0.9 copy-start.12
  5.5 21.7 %collective-permute-start.8 = (bf16[2,2,128,128]{3,2,1,0:T(8,128)(2,1)S(1)}, bf16[2,2,128,128]{3,2,1,0:T(8,128)(2,1)S(1)}, u32[]{:S(2)}, u32[]{:S(2)}) collective-permute-start(bf16[2,2,128,128]{3,2,1,0:T(8,128)(2,1)S(1)} %pack.3), channel_id=1, source_target_pairs={{0,16},{4,20},{8,24},{12,28},{16,0},{20,4},{24,8},{28,12},{1,17},{... | collective-permute-start | bytes 393224 | tf_op jit(solution)/shard_map/ppermute | solution.py:301
  8.1 19.1 %collective-permute-start.9 = (bf16[2,2,128,128]{3,2,1,0:T(8,128)(2,1)S(1)}, bf16[2,2,128,128]{3,2,1,0:T(8,128)(2,1)S(1)}, u32[]{:S(2)}, u32[]{:S(2)}) collective-permute-start(bf16[2,2,128,128]{3,2,1,0:T(8,128)(2,1)S(1)} %pack.3), channel_id=1, source_target_pairs={{0,24},{4,28},{8,0},{12,4},{16,8},{20,12},{24,16},{28,20},{1,25},{... | collective-permute-start | bytes 393224 | tf_op jit(solution)/shard_map/ppermute | solution.py:301
  8.6 18.6 %collective-permute-start.7 = (bf16[2,2,128,128]{3,2,1,0:T(8,128)(2,1)S(1)}, bf16[2,2,128,128]{3,2,1,0:T(8,128)(2,1)S(1)}, u32[]{:S(2)}, u32[]{:S(2)}) collective-permute-start(bf16[2,2,128,128]{3,2,1,0:T(8,128)(2,1)S(1)} %pack.3), channel_id=1, source_target_pairs={{0,8},{4,12},{8,16},{12,20},{16,24},{20,28},{24,0},{28,4},{1,9},{5... | collective-permute-start | bytes 393224 | tf_op jit(solution)/shard_map/ppermute | solution.py:301
  27.3 13.9 %collective-permute-start.10 = (bf16[4,2,2,128,128]{4,3,2,1,0:T(8,128)(2,1)S(1)}, bf16[4,2,2,128,128]{4,3,2,1,0:T(8,128)(2,1)}, u32[]{:S(2)}, u32[]{:S(2)}) collective-permute-start(bf16[4,2,2,128,128]{4,3,2,1,0:T(8,128)(2,1)S(1)} %pad_maximum_fusion.refs_2_), channel_id=1, source_target_pairs={{0,4},{4,0},{8,12},{12,8},{16,20},{20,16},{24,28},{28,24},{1,5},{5... | collective-permute-start | bytes 1572872 | tf_op jit(solution)/shard_map/ppermute | solution.py:301
  28.9 12.8 %copy-start.7 = (bf16[8,2,128,128]{3,2,1,0:T(8,128)(2,1)}, bf16[8,2,128,128]{3,2,1,0:T(8,128)(2,1)S(1)}, u32[]{:S(2)}) copy-start(bf16[8,2,128,128]{3,2,1,0:T(8,128)(2,1)S(1)} %collective-permute-done.refs_2_) | copy-start | bytes 1572868
  28.9 14.9 %collective-permute-start.1 = (bf16[8,2,128,128]{3,2,1,0:T(8,128)(2,1)S(1)}, bf16[8,2,128,128]{3,2,1,0:T(8,128)(2,1)S(1)}, u32[]{:S(2)}, u32[]{:S(2)}) collective-permute-start(bf16[8,2,128,128]{3,2,1,0:T(8,128)(2,1)S(1)} %collective-permute-done.refs_2_), channel_id=1, source_target_pairs={{8,16},{12,20},{16,24},{20,28},{9,17},{13,21},{17,25},{21,29},{10,... | collective-permute-start | bytes 1572872 | tf_op jit(solution)/shard_map/ppermute | solution.py:301
  30.2 22.3 %collective-permute-start.17 = (bf16[8,2,128,128]{3,2,1,0:T(8,128)(2,1)S(1)}, bf16[8,2,128,128]{3,2,1,0:T(8,128)(2,1)S(1)}, u32[]{:S(2)}, u32[]{:S(2)}) collective-permute-start(bf16[8,2,128,128]{3,2,1,0:T(8,128)(2,1)S(1)} %pack.2.refs_0_), channel_id=1, source_target_pairs={{0,4},{8,12},{16,20},{24,28},{1,5},{9,13},{17,21},{25,29},{2,6},{1... | collective-permute-start | bytes 1572872 | tf_op jit(solution)/shard_map/ppermute | solution.py:301
  32.6 20.6 %collective-permute-start.11 = (bf16[4,2,2,128,128]{4,3,2,1,0:T(8,128)(2,1)S(1)}, bf16[4,2,2,128,128]{4,3,2,1,0:T(8,128)(2,1)}, u32[]{:S(2)}, u32[]{:S(2)}) collective-permute-start(bf16[4,2,2,128,128]{4,3,2,1,0:T(8,128)(2,1)S(1)} %pad_maximum_fusion.refs_2_), channel_id=1, source_target_pairs={{0,2},{1,3},{2,0},{3,1},{4,6},{5,7},{6,4},{7,5},{8,10},{9,11},{10,... | collective-permute-start | bytes 1572872 | tf_op jit(solution)/shard_map/ppermute | solution.py:301
  41.2 16.5 %collective-permute-start.12 = (bf16[4,2,2,128,128]{4,3,2,1,0:T(8,128)(2,1)}, bf16[4,2,2,128,128]{4,3,2,1,0:T(8,128)(2,1)}, u32[]{:S(2)}, u32[]{:S(2)}) collective-permute-start(bf16[4,2,2,128,128]{4,3,2,1,0:T(8,128)(2,1)} %collective-permute-done.10.refs_3_), channel_id=1, source_target_pairs={{0,2},{1,3},{2,0},{3,1},{4,6},{5,7},{6,4},{7,5},{8,10},{9,11},{10,... | collective-permute-start | bytes 1572872 | tf_op jit(solution)/shard_map/ppermute | solution.py:301
  43.8 14.2 %collective-permute-start.3 = (bf16[8,2,128,128]{3,2,1,0:T(8,128)(2,1)S(1)}, bf16[8,2,128,128]{3,2,1,0:T(8,128)(2,1)S(1)}, u32[]{:S(2)}, u32[]{:S(2)}) collective-permute-start(bf16[8,2,128,128]{3,2,1,0:T(8,128)(2,1)S(1)} %collective-permute-done.1.refs_1_), channel_id=1, source_target_pairs={{16,24},{20,28},{17,25},{21,29},{18,26},{22,30},{19,27},{23,31}} | collective-permute-start | bytes 1572872 | tf_op jit(solution)/shard_map/ppermute | solution.py:301
  45.1 17.6 %collective-permute-start.2 = (bf16[8,2,128,128]{3,2,1,0:T(8,128)(2,1)S(1)}, bf16[8,2,128,128]{3,2,1,0:T(8,128)(2,1)S(1)}, u32[]{:S(2)}, u32[]{:S(2)}) collective-permute-start(bf16[8,2,128,128]{3,2,1,0:T(8,128)(2,1)S(1)} %collective-permute-done.1.refs_1_), channel_id=1, source_target_pairs={{16,20},{20,16},{24,28},{28,24},{17,21},{21,17},{25,29},{29,25},{1... | collective-permute-start | bytes 1572872 | tf_op jit(solution)/shard_map/ppermute | solution.py:301
  47.5 0.8 copy-start.1
  52.4 0.8 copy-start.9
  53.2 10.9 %collective-permute-start.13 = (bf16[4,2,2,128,128]{4,3,2,1,0:T(8,128)(2,1)S(1)}, bf16[4,2,2,128,128]{4,3,2,1,0:T(8,128)(2,1)S(1)}, u32[]{:S(2)}, u32[]{:S(2)}) collective-permute-start(bf16[4,2,2,128,128]{4,3,2,1,0:T(8,128)(2,1)S(1)} %pad_maximum_fusion.refs_2_), channel_id=1, source_target_pairs={{0,1},{1,0},{2,3},{3,2},{4,5},{5,4},{6,7},{7,6},{8,9},{9,8},{10,11... | collective-permute-start | bytes 1572872 | tf_op jit(solution)/shard_map/ppermute | solution.py:301
  53.2 20.3 %collective-permute-start.6 = (bf16[8,2,128,128]{3,2,1,0:T(8,128)(2,1)}, bf16[8,2,128,128]{3,2,1,0:T(8,128)(2,1)S(1)}, u32[]{:S(2)}, u32[]{:S(2)}) collective-permute-start(bf16[8,2,128,128]{3,2,1,0:T(8,128)(2,1)} %copy-done.7), channel_id=1, source_target_pairs={{8,12},{12,8},{16,20},{20,16},{24,28},{28,24},{9,13},{13,9},{17,21... | collective-permute-start | bytes 1572872 | tf_op jit(solution)/shard_map/ppermute | solution.py:301
  57.6 28.0 %collective-permute-start.14 = (bf16[4,2,2,128,128]{4,3,2,1,0:T(8,128)(2,1)}, bf16[4,2,2,128,128]{4,3,2,1,0:T(8,128)(2,1)}, u32[]{:S(2)}, u32[]{:S(2)}) collective-permute-start(bf16[4,2,2,128,128]{4,3,2,1,0:T(8,128)(2,1)} %collective-permute-done.10.refs_3_), channel_id=1, source_target_pairs={{0,1},{1,0},{2,3},{3,2},{4,5},{5,4},{6,7},{7,6},{8,9},{9,8},{10,11... | collective-permute-start | bytes 1572872 | tf_op jit(solution)/shard_map/ppermute | solution.py:301
  57.9 27.7 %collective-permute-start.15 = (bf16[4,2,2,128,128]{4,3,2,1,0:T(8,128)(2,1)}, bf16[4,2,2,128,128]{4,3,2,1,0:T(8,128)(2,1)}, u32[]{:S(2)}, u32[]{:S(2)}) collective-permute-start(bf16[4,2,2,128,128]{4,3,2,1,0:T(8,128)(2,1)} %collective-permute-done.11.refs_4_), channel_id=1, source_target_pairs={{0,1},{1,0},{2,3},{3,2},{4,5},{5,4},{6,7},{7,6},{8,9},{9,8},{10,11... | collective-permute-start | bytes 1572872 | tf_op jit(solution)/shard_map/ppermute | solution.py:301
  62.6 23.0 %collective-permute-start.16 = (bf16[4,2,2,128,128]{4,3,2,1,0:T(8,128)(2,1)}, bf16[4,2,2,128,128]{4,3,2,1,0:T(8,128)(2,1)}, u32[]{:S(2)}, u32[]{:S(2)}) collective-permute-start(bf16[4,2,2,128,128]{4,3,2,1,0:T(8,128)(2,1)} %collective-permute-done.12.refs_5_), channel_id=1, source_target_pairs={{0,1},{1,0},{2,3},{3,2},{4,5},{5,4},{6,7},{7,6},{8,9},{9,8},{10,11... | collective-permute-start | bytes 1572872 | tf_op jit(solution)/shard_map/ppermute | solution.py:301
  64.1 21.6 %copy-start.16 = (s32[1,1,8]{2,1,0:T(1,128)S(1)}, s32[1,1,8]{2,1,0:T(1,128)}, u32[]{:S(2)}) copy-start(s32[1,1,8]{2,1,0:T(1,128)} %param.13) | copy-start | bytes 100
  64.1 21.6 %copy-start.18 = (s32[1,1,8]{2,1,0:T(1,128)S(1)}, s32[1,1,8]{2,1,0:T(1,128)}, u32[]{:S(2)}) copy-start(s32[1,1,8]{2,1,0:T(1,128)} %param.14) | copy-start | bytes 100
  64.1 0.8 copy-start.3
  64.9 33.4 %collective-permute-start.4 = (bf16[4,2,128,128]{3,2,1,0:T(8,128)(2,1)}, bf16[4,2,128,128]{3,2,1,0:T(8,128)(2,1)}, u32[]{:S(2)}, u32[]{:S(2)}) collective-permute-start(bf16[4,2,128,128]{3,2,1,0:T(8,128)(2,1)} %slice.8), channel_id=1, source_target_pairs={{24,28},{28,24},{25,29},{29,25},{26,30},{30,26},{27,31},{31,27}} | collective-permute-start | bytes 786440 | tf_op jit(solution)/shard_map/ppermute | solution.py:301
  73.6 0.8 copy-start.5
  74.4 23.9 %collective-permute-start.5 = (bf16[4,2,128,128]{3,2,1,0:T(8,128)(2,1)}, bf16[4,2,128,128]{3,2,1,0:T(8,128)(2,1)}, u32[]{:S(2)}, u32[]{:S(2)}) collective-permute-start(bf16[4,2,128,128]{3,2,1,0:T(8,128)(2,1)} %slice.9), channel_id=1, source_target_pairs={{16,24},{20,28},{17,25},{21,29},{18,26},{22,30},{19,27},{23,31}} | collective-permute-start | bytes 786440 | tf_op jit(solution)/shard_map/ppermute | solution.py:301
  75.7 10.0 %copy-start.2 = (bf16[8,2,128,128]{3,2,1,0:T(8,128)(2,1)S(1)}, bf16[8,2,128,128]{3,2,1,0:T(8,128)(2,1)}, u32[]{:S(2)}) copy-start(bf16[8,2,128,128]{3,2,1,0:T(8,128)(2,1)} %copy-done.1) | copy-start | bytes 1572868
  75.7 10.0 %copy-start.4 = (bf16[4,2,2,128,128]{4,3,2,1,0:T(8,128)(2,1)S(1)}, bf16[4,2,2,128,128]{4,3,2,1,0:T(8,128)(2,1)}, u32[]{:S(2)}) copy-start(bf16[4,2,2,128,128]{4,3,2,1,0:T(8,128)(2,1)} %copy-done.3) | copy-start | bytes 1572868
  75.7 10.0 %copy-start.6 = (bf16[8,2,128,128]{3,2,1,0:T(8,128)(2,1)S(1)}, bf16[8,2,128,128]{3,2,1,0:T(8,128)(2,1)}, u32[]{:S(2)}) copy-start(bf16[8,2,128,128]{3,2,1,0:T(8,128)(2,1)} %copy-done.5) | copy-start | bytes 1572868
  76.5 1.0 %copy-start.8 = (bf16[8,2,128,128]{3,2,1,0:T(8,128)(2,1)S(1)}, bf16[8,2,128,128]{3,2,1,0:T(8,128)(2,1)}, u32[]{:S(2)}) copy-start(bf16[8,2,128,128]{3,2,1,0:T(8,128)(2,1)} %copy-done.7) | copy-start | bytes 1572868
  77.6 1.0 %copy-start.10 = (bf16[8,2,128,128]{3,2,1,0:T(8,128)(2,1)S(1)}, bf16[8,2,128,128]{3,2,1,0:T(8,128)(2,1)}, u32[]{:S(2)}) copy-start(bf16[8,2,128,128]{3,2,1,0:T(8,128)(2,1)} %copy-done.9) | copy-start | bytes 1572868
  78.6 0.7 copy-start.15
  79.3 0.7 copy-start.17

commit v2 on v1

--- a/solution.py
+++ b/solution.py
@@ -24,26 +24,53 @@
 exponent_scale = math.log2(math.e) / math.sqrt(HEAD_DIM)
 
 
-def pack_kernel(heads, first_ref, key_ref, value_ref, out_ref):
-    for n in range(heads):
-        lanes = pl.ds(pl.multiple_of((first_ref[0] + n) * HEAD_DIM, HEAD_DIM), HEAD_DIM)
-        out_ref[n, 0] = key_ref[:, lanes]
-        out_ref[n, 1] = value_ref[:, lanes].T
-
-
-def pack(keys, values, first_head, heads):
-    inside = pl.BlockSpec(memory_space=pltpu.VMEM)
+def pack_kernel(first_ref, *refs):
+    sources, outs = refs[:4], refs[4:6]
+    wides, narrows, semaphores = refs[6], refs[7], refs[8]
+    heads = outs[1].shape[0]
+    lanes = pl.ds(pl.multiple_of(first_ref[0] * HEAD_DIM, HEAD_DIM), heads * HEAD_DIM)
+    copies = [
+        pltpu.make_async_copy(sources[n].at[:, lanes], narrows.at[n], semaphores.at[n])
+        for n in range(2)
+    ] + [
+        pltpu.make_async_copy(sources[n + 2], wides.at[n], semaphores.at[n + 2])
+        for n in range(2)
+    ]
+    for copy in copies:
+        copy.start()
+    for out, held, pair in ((outs[1], narrows, copies[:2]), (outs[0], wides, copies[2:])):
+        for copy in pair:
+            copy.wait()
+        for n in range(out.shape[0]):
+            out[n, 0] = held[0, :, n * HEAD_DIM : (n + 1) * HEAD_DIM]
+            out[n, 1] = held[1, :, n * HEAD_DIM : (n + 1) * HEAD_DIM].T
+
+
+def pack(suffix_keys, suffix_values, prefix_keys, prefix_values, first_head, heads):
+    kind = suffix_keys.dtype
+    width = KV_HEADS * HEAD_DIM
     return pl.pallas_call(
-        functools.partial(pack_kernel, heads),
-        out_shape=pltpu.VMEM((heads, 2, BLOCK, HEAD_DIM), keys.dtype),
-        in_specs=[pl.BlockSpec(memory_space=pltpu.SMEM), inside, inside],
-        out_specs=inside,
-        compiler_params=pltpu.CompilerParams(vmem_limit_bytes=4 * 2**20),
+        pack_kernel,
+        out_shape=(
+            pltpu.VMEM((KV_HEADS, 2, BLOCK, HEAD_DIM), kind),
+            pltpu.VMEM((heads, 2, BLOCK, HEAD_DIM), kind),
+        ),
+        in_specs=[pl.BlockSpec(memory_space=pltpu.SMEM)]
+        + [pl.BlockSpec(memory_space=pltpu.HBM)] * 4,
+        out_specs=[pl.BlockSpec(memory_space=pltpu.VMEM)] * 2,
+        scratch_shapes=[
+            pltpu.VMEM((2, BLOCK, width), kind),
+            pltpu.VMEM((2, BLOCK, heads * HEAD_DIM), kind),
+            pltpu.SemaphoreType.DMA((4,)),
+        ],
+        compiler_params=pltpu.CompilerParams(vmem_limit_bytes=6 * 2**20),
         name="pack",
     )(
         first_head,
-        pltpu.with_memory_space_constraint(keys, pltpu.VMEM),
-        pltpu.with_memory_space_constraint(values, pltpu.VMEM),
+        *(
+            pltpu.with_memory_space_constraint(x, pltpu.HBM)
+            for x in (prefix_keys, prefix_values, suffix_keys, suffix_values)
+        ),
     )
 
 
@@ -301,25 +328,23 @@
         return lax.ppermute(value, axis, pairs)
 
     swap_columns = [(i, i ^ 1) for i in range(seq_count)]
-    own = pack(suffix_keys[0], suffix_values[0], jnp.zeros(1, jnp.int32), KV_HEADS)
     first_head = (samp_index * per_share).astype(jnp.int32)
-    own_share = pack(prefix_keys, prefix_values, first_head[None], per_share)
+    own, own_share = pack(
+        suffix_keys[0], suffix_values[0], prefix_keys, prefix_values, first_head[None], per_share
+    )
 
     held = {(0, False): own}
+    top = rows - 1
     across = [(z * COLUMNS, z * COLUMNS + 1) for z in range(rows)]
     held[0, True] = move(own, across)
     for k in range(1, rows):
-        upward = along_rows([(z, z + 1) for z in range(k - 1, rows - 1)])
-        held[k, False] = move(held[k - 1, False], upward)
-        if k < rows - 1:
+        upward = along_rows([(z, z + 1) for z in range(k - 1, top)])
+        if k < top or top == 1:
+            held[k, False] = move(held[k - 1, False], upward)
             held[k, True] = move(held[k, False], swap_columns[k * COLUMNS :])
-    low = slice(0, KV_HEADS // 2)
-    high = slice(KV_HEADS // 2, KV_HEADS)
-    top = rows - 1
-    from_side = move(held[top, False][low], swap_columns[top * COLUMNS :])
-    source = held[top - 1, True] if top > 1 else move(own, [(1, 0)] + across[:1])
-    from_below = move(source[high], along_rows([(top - 1, top)]))
-    held[top, True] = (from_side, from_below)
+        else:
+            held[k, False] = move(held[1, False], along_rows([(1, top)]))
+            held[k, True] = move(held[1, True], along_rows([(1, top)]))
 
     gathered = [own_share]
     for k in range(1, rows):
@@ -334,8 +359,8 @@
     near = [same, other, same_x, other_x]
     far = [move(piece, swap_core, "samp") for piece in near]
 
-    early, late = stages(rows)
-    middle = [slot for slot in held if slot not in early and slot not in late]
+    early, late, latest = stages(rows)
+    middle = [slot for slot in held if slot not in early + late + latest]
     tables = (
         jnp.stack([seq_index, samp_index]).astype(jnp.int32),
         layout_pre[0, 0],
@@ -349,15 +374,16 @@
 
     state = run(early, [], None, False)
     state = run(middle, near + far, state, False)
-    return run(late, [], state, True)[None]
+    if late:
+        state = run(late, [], state, False)
+    return run(latest, [], state, True)[None]
 
 
 def stages(rows):
     early = [(0, False), (0, True)] + [(1, False)] * (rows > 2)
-    late = [(rows - 1, False), (rows - 1, True)]
-    if rows > 2:
-        late.insert(0, (rows - 2, True))
-    return early, [slot for slot in late if slot not in early]
+    late = [(rows - 2, True), (rows - 1, False)] if rows > 2 else []
+    latest = [(rows - 1, True)] + [(rows - 1, False)] * (rows <= 2)
+    return early, late, latest
 
 
 def solution(mesh):

time: 104 us -> 93 us (0.89)
  starting transfers between devices: 28.5 us -> 21.9 us
  local copies, waits for them, and re-layouts: 12 us -> 5.82 us
  Pallas kernels: 23.6 us -> 26.4 us
    ppermute x18 -> x17, starting transfers between devices: 28.5 us -> 21.9 us  [move(): return lax.ppermute(value, axis, pairs)]
    unnamed x38 -> x26, local copies, waits for them, and re-layouts: 10.5 us -> 5.82 us
    pallas_call x3 -> x4, Pallas kernels: 23.3 us -> 25 us  [attend(): pl.pallas_call(functools.partial(attend_kernel, (plan, prefix_count, rows...]
    slice x2 -> x0, local copies, waits for them, and re-layouts: 1.45 us -> none  [the longest x1 0.72 us: shards(): from_below = move(source[high], along_rows([(top - 1, top)]))]
    pallas_call x2 -> x1, Pallas kernels: 0.28 us -> 1.4 us  [pack(): pl.pallas_call(pack_kernel, out_shape=(pltpu.VMEM((KV_HEADS, 2, BLOCK, HE...]
    ppermute x18 -> x17, waiting for transfers between devices: 38.1 us -> 37.3 us  [move(): return lax.ppermute(value, axis, pairs)]
  transfers between devices with their start and end apart: 18 -> 17, of which waited for: 6 -> 8; matrix products, arithmetic and copies ran while one was open for 2% -> 0% of each run, Pallas kernels for 18% -> 22%
where the time goes in v2:
time: 93 us; the launch traced here: 92.6 us
  waiting for transfers between devices  37.3 us (40%)
  Pallas kernels  26.4 us (28%)
  starting transfers between devices  21.9 us (24%)
  local copies, waits for them, and re-layouts  5.82 us (6%)
  between operations  1.01 us (1%)
    ppermute x17, waiting for transfers between devices, move(): return lax.ppermute(value, axis, pairs)  37.3 us
    pallas_call x4, Pallas kernels, attend(): pl.pallas_call(functools.partial(attend_kernel, (plan, prefix_count, rows...  25 us
    ppermute x17, starting transfers between devices, move(): return lax.ppermute(value, axis, pairs)  21.9 us
    unnamed x26, local copies, waits for them, and re-layouts  5.82 us
  transfers between devices with their start and end apart: 17, of which 8 were waited for; matrix products, arithmetic and copies ran while one was open for 0% of the time, Pallas kernels for 22%

profile of v2, /device:TPU:26, one launch (start us, length us, event | category | flops | bytes accessed | tf_op | source)
XLA Modules:
  0.0 92.6 jit_solution(18153289117950491875)
XLA Ops:
  0.0 1.4 %pack.1 = (bf16[8,2,128,128]{3,2,1,0:T(8,128)(2,1)S(1)}, bf16[2,2,128,128]{3,2,1,0:T(8,128)(2,1)S(1)}) custom-call(s32[1]{0:T(128)} %bitcast.5.first_ref, bf16[128,1024]{1,0:T(8,128)(2,1)} %refs_0_.1, bf16[128,1024]{1,0:T(8,128)(2,1)} %refs_1_.1, bf16[128,1024]{1,0:T(8,128)(2,1)} %bitcast.26, bf16[128,1024]{1,0:T(8,128)(2,1)} %bitcast.27), custom_call_target="tpu_custom_call" | custom-call | tf_op jit(solution)/shard_map/pack/pallas_call | solution.py:52
  1.4 0.4 collective-permute-start.7
  1.8 0.4 collective-permute-start.8
  2.3 3.4 %collective-permute-start.6 = (bf16[2,2,128,128]{3,2,1,0:T(8,128)(2,1)S(1)}, bf16[2,2,128,128]{3,2,1,0:T(8,128)(2,1)S(1)}, u32[]{:S(2)}, u32[]{:S(2)}) collective-permute-start(bf16[2,2,128,128]{3,2,1,0:T(8,128)(2,1)S(1)} %get-tuple-element.8), channel_id=1, source_target_pairs={{0,8},{4,12},{8,16},{12,20},{16,24},{20,28},{24,0},{28,4},{1,9},{5... | collective-permute-start | bytes 393224 | tf_op jit(solution)/shard_map/ppermute | solution.py:328
  5.6 7.6 %collective-permute-done.7 = bf16[2,2,128,128]{3,2,1,0:T(8,128)(2,1)S(1)} collective-permute-done((bf16[2,2,128,128]{3,2,1,0:T(8,128)(2,1)S(1)}, bf16[2,2,128,128]{3,2,1,0:T(8,128)(2,1)S(1)}, u32[]{:S(2)}, u32[]{:S(2)}) %collective-permute-start.7) | collective-permute-done | bytes 131104 | tf_op jit(solution)/shard_map/ppermute | solution.py:328
  13.3 0.0 collective-permute-done.8
  13.3 0.2 collective-permute-done.6
  13.5 0.1 pad_maximum_fusion.refs_2_
  13.6 0.0 copy-start.10
  13.6 0.0 copy-start.12
  13.6 1.6 %collective-permute-start.9 = (bf16[4,2,2,128,128]{4,3,2,1,0:T(8,128)(2,1)S(1)}, bf16[4,2,2,128,128]{4,3,2,1,0:T(8,128)(2,1)S(1)}, u32[]{:S(2)}, u32[]{:S(2)}) collective-permute-start(bf16[4,2,2,128,128]{4,3,2,1,0:T(8,128)(2,1)S(1)} %pad_maximum_fusion.refs_2_), channel_id=1, source_target_pairs={{0,4},{4,0},{8,12},{12,8},{16,20},{20,16},{24,28},{28,24},{1,5},{5... | collective-permute-start | bytes 1572872 | tf_op jit(solution)/shard_map/ppermute | solution.py:328
  15.2 1.3 %collective-permute-start = (bf16[8,2,128,128]{3,2,1,0:T(8,128)(2,1)S(1)}, bf16[8,2,128,128]{3,2,1,0:T(8,128)(2,1)}, u32[]{:S(2)}, u32[]{:S(2)}) collective-permute-start(bf16[8,2,128,128]{3,2,1,0:T(8,128)(2,1)S(1)} %get-tuple-element.7.refs_0_), channel_id=1, source_target_pairs={{0,8},{4,12},{8,16},{12,20},{16,24},{20,28},{1,9},{5,13},{9,17},{1... | collective-permute-start | bytes 1572872 | tf_op jit(solution)/shard_map/ppermute | solution.py:328
  16.5 2.4 %collective-permute-start.16 = (bf16[8,2,128,128]{3,2,1,0:T(8,128)(2,1)S(1)}, bf16[8,2,128,128]{3,2,1,0:T(8,128)(2,1)S(1)}, u32[]{:S(2)}, u32[]{:S(2)}) collective-permute-start(bf16[8,2,128,128]{3,2,1,0:T(8,128)(2,1)S(1)} %get-tuple-element.7.refs_0_), channel_id=1, source_target_pairs={{0,4},{8,12},{16,20},{24,28},{1,5},{9,13},{17,21},{25,29},{2,6},{1... | collective-permute-start | bytes 1572872 | tf_op jit(solution)/shard_map/ppermute | solution.py:328
  18.9 0.6 collective-permute-start.10
  19.5 0.0 collective-permute-start.12
  19.5 8.0 %collective-permute-done.9.refs_3_ = bf16[4,2,2,128,128]{4,3,2,1,0:T(8,128)(2,1)S(1)} collective-permute-done((bf16[4,2,2,128,128]{4,3,2,1,0:T(8,128)(2,1)S(1)}, bf16[4,2,2,128,128]{4,3,2,1,0:T(8,128)(2,1)S(1)}, u32[]{:S(2)}, u32[]{:S(2)}) %collective-permute-start.9) | collective-permute-done | bytes 524320 | tf_op jit(solution)/shard_map/ppermute | solution.py:328
  27.5 0.5 collective-permute-start.11
  28.0 4.0 %collective-permute-done.refs_2_ = bf16[8,2,128,128]{3,2,1,0:T(8,128)(2,1)} collective-permute-done((bf16[8,2,128,128]{3,2,1,0:T(8,128)(2,1)S(1)}, bf16[8,2,128,128]{3,2,1,0:T(8,128)(2,1)}, u32[]{:S(2)}, u32[]{:S(2)}) %collective-permute-start) | collective-permute-done | bytes 524320 | tf_op jit(solution)/shard_map/ppermute | solution.py:328
  32.0 2.4 %collective-permute-start.1 = (bf16[8,2,128,128]{3,2,1,0:T(8,128)(2,1)}, bf16[8,2,128,128]{3,2,1,0:T(8,128)(2,1)S(1)}, u32[]{:S(2)}, u32[]{:S(2)}) collective-permute-start(bf16[8,2,128,128]{3,2,1,0:T(8,128)(2,1)} %collective-permute-done.refs_2_), channel_id=1, source_target_pairs={{8,12},{12,8},{16,20},{20,16},{24,28},{28,24},{9,13},{13,9},{17,21... | collective-permute-start | bytes 1572872 | tf_op jit(solution)/shard_map/ppermute | solution.py:328
  34.5 4.3 %collective-permute-done.16.refs_1_ = bf16[8,2,128,128]{3,2,1,0:T(8,128)(2,1)S(1)} collective-permute-done((bf16[8,2,128,128]{3,2,1,0:T(8,128)(2,1)S(1)}, bf16[8,2,128,128]{3,2,1,0:T(8,128)(2,1)S(1)}, u32[]{:S(2)}, u32[]{:S(2)}) %collective-permute-start.16) | collective-permute-done | bytes 524320 | tf_op jit(solution)/shard_map/ppermute | solution.py:328
  38.7 0.8 copy-done.7
  39.6 1.3 %collective-permute-start.3 = (bf16[8,2,128,128]{3,2,1,0:T(8,128)(2,1)}, bf16[8,2,128,128]{3,2,1,0:T(8,128)(2,1)}, u32[]{:S(2)}, u32[]{:S(2)}) collective-permute-start(bf16[8,2,128,128]{3,2,1,0:T(8,128)(2,1)} %collective-permute-done.refs_2_), channel_id=1, source_target_pairs={{8,16},{12,20},{16,24},{20,28},{9,17},{13,21},{17,25},{21,29},{10,... | collective-permute-start | bytes 1572872 | tf_op jit(solution)/shard_map/ppermute | solution.py:328
  40.8 0.0 collective-permute-done.10.refs_4_
  40.8 0.1 collective-permute-start.13
  40.9 0.0 collective-permute-done.12.refs_6_
  40.9 0.0 copy-start.1
  41.0 0.8 copy-done.1
  41.7 0.5 collective-permute-start.14
  42.2 1.1 %collective-permute-done.11.refs_5_ = bf16[4,2,2,128,128]{4,3,2,1,0:T(8,128)(2,1)} collective-permute-done((bf16[4,2,2,128,128]{4,3,2,1,0:T(8,128)(2,1)S(1)}, bf16[4,2,2,128,128]{4,3,2,1,0:T(8,128)(2,1)}, u32[]{:S(2)}, u32[]{:S(2)}) %collective-permute-start.11) | collective-permute-done | bytes 524320 | tf_op jit(solution)/shard_map/ppermute | solution.py:328
  43.3 0.0 collective-permute-start.15
  43.3 5.5 %collective-permute-done.1.refs_0_ = bf16[8,2,128,128]{3,2,1,0:T(8,128)(2,1)S(1)} collective-permute-done((bf16[8,2,128,128]{3,2,1,0:T(8,128)(2,1)}, bf16[8,2,128,128]{3,2,1,0:T(8,128)(2,1)S(1)}, u32[]{:S(2)}, u32[]{:S(2)}) %collective-permute-start.1) | collective-permute-done | bytes 524320 | tf_op jit(solution)/shard_map/ppermute | solution.py:328
  48.8 1.3 %collective-permute-start.5 = (bf16[8,2,128,128]{3,2,1,0:T(8,128)(2,1)}, bf16[8,2,128,128]{3,2,1,0:T(8,128)(2,1)}, u32[]{:S(2)}, u32[]{:S(2)}) collective-permute-start(bf16[8,2,128,128]{3,2,1,0:T(8,128)(2,1)} %collective-permute-done.refs_2_), channel_id=1, source_target_pairs={{8,24},{12,28},{9,25},{13,29},{10,26},{14,30},{11,27},{15,31}} | collective-permute-start | bytes 1572872 | tf_op jit(solution)/shard_map/ppermute | solution.py:328
  50.1 6.6 %collective-permute-done.3.refs_1_ = bf16[8,2,128,128]{3,2,1,0:T(8,128)(2,1)} collective-permute-done((bf16[8,2,128,128]{3,2,1,0:T(8,128)(2,1)}, bf16[8,2,128,128]{3,2,1,0:T(8,128)(2,1)}, u32[]{:S(2)}, u32[]{:S(2)}) %collective-permute-start.3) | collective-permute-done | bytes 524320 | tf_op jit(solution)/shard_map/ppermute | solution.py:328
  56.7 4.4 %collective-permute-start.4 = (bf16[8,2,128,128]{3,2,1,0:T(8,128)(2,1)}, bf16[8,2,128,128]{3,2,1,0:T(8,128)(2,1)}, u32[]{:S(2)}, u32[]{:S(2)}) collective-permute-start(bf16[8,2,128,128]{3,2,1,0:T(8,128)(2,1)} %collective-permute-done.3.refs_1_), channel_id=1, source_target_pairs={{16,20},{20,16},{24,28},{28,24},{17,21},{21,17},{25,29},{29,25},{1... | collective-permute-start | bytes 1572872 | tf_op jit(solution)/shard_map/ppermute | solution.py:328
  61.1 0.0 collective-permute-done.13.refs_7_
  61.1 0.8 copy-done.3
  61.9 1.3 %collective-permute-start.2 = (bf16[8,2,128,128]{3,2,1,0:T(8,128)(2,1)S(1)}, bf16[8,2,128,128]{3,2,1,0:T(8,128)(2,1)}, u32[]{:S(2)}, u32[]{:S(2)}) collective-permute-start(bf16[8,2,128,128]{3,2,1,0:T(8,128)(2,1)S(1)} %collective-permute-done.1.refs_0_), channel_id=1, source_target_pairs={{8,24},{12,28},{9,25},{13,29},{10,26},{14,30},{11,27},{15,31}} | collective-permute-start | bytes 1572872 | tf_op jit(solution)/shard_map/ppermute | solution.py:328
  63.2 0.0 copy-start.2
  63.9 0.1 pad_add_fusion.place
  64.0 1.0 %copy-done.6 = bf16[8,2,128,128]{3,2,1,0:T(8,128)(2,1)S(1)} copy-done((bf16[8,2,128,128]{3,2,1,0:T(8,128)(2,1)S(1)}, bf16[8,2,128,128]{3,2,1,0:T(8,128)(2,1)}, u32[]{:S(2)}) %copy-start.6) | copy-done | bytes 524312
  65.1 1.0 %copy-done.8 = bf16[8,2,128,128]{3,2,1,0:T(8,128)(2,1)S(1)} copy-done((bf16[8,2,128,128]{3,2,1,0:T(8,128)(2,1)S(1)}, bf16[8,2,128,128]{3,2,1,0:T(8,128)(2,1)}, u32[]{:S(2)}) %copy-start.8) | copy-done | bytes 524312
  66.1 0.7 copy-done.9
  66.8 0.7 copy-done.11
  67.4 6.2 %shard_map.82.refs_10_ = f32[8,144,640]{2,1,0:T(8,128)S(1)} custom-call(s32[2]{0:T(128)S(1)} %pad_add_fusion.place, s32[8]{0:T(128)S(1)} %bitcast.18, s32[8]{0:T(128)S(1)} %bitcast.22, s32[1]{0:T(128)S(6)} %copy.13.lengths, bf16[128,5120]{1,0:T(8,128)(2,1)S(1)} %bitcast.13, bf16[8,2,128,128]{3,2,1,0:T(8,128)(2,1)S(1)} %copy-done.6, ...), custom_call_target="tpu_custom_call" | custom-call | tf_op jit(solution)/shard_map/pallas_call | solution.py:297
  73.7 12.4 %shard_map.83.refs_2_ = f32[8,144,640]{2,1,0:T(8,128)S(1)} custom-call(s32[2]{0:T(128)S(1)} %pad_add_fusion.place, s32[8]{0:T(128)S(1)} %bitcast.19, s32[8]{0:T(128)S(1)} %bitcast.23, s32[1]{0:T(128)S(6)} %copy.13.lengths, bf16[128,5120]{1,0:T(8,128)(2,1)S(1)} %bitcast.14, ...), custom_call_target="tpu_custom_call", output_to_operand_aliasing={{}: (15, {})} | custom-call | tf_op jit(solution)/shard_map/pallas_call | solution.py:297
  86.1 1.5 %shard_map.84.refs_1_ = f32[8,144,640]{2,1,0:T(8,128)S(1)} custom-call(s32[2]{0:T(128)S(1)} %pad_add_fusion.place, s32[8]{0:T(128)S(1)} %bitcast.20, s32[8]{0:T(128)S(1)} %bitcast.24, s32[1]{0:T(128)S(6)} %copy.13.lengths, bf16[128,5120]{1,0:T(8,128)(2,1)S(1)} %bitcast.15, ...), custom_call_target="tpu_custom_call", output_to_operand_aliasing={{}: (7, {})} | custom-call | tf_op jit(solution)/shard_map/pallas_call | solution.py:297
  87.5 0.0 collective-permute-done.2.refs_0_
  87.5 5.0 %shard_map.85 = bf16[128,5120]{1,0:T(8,128)(2,1)} custom-call(s32[2]{0:T(128)S(1)} %pad_add_fusion.place, s32[8]{0:T(128)S(1)} %bitcast.21, s32[8]{0:T(128)S(1)} %bitcast.25, s32[1]{0:T(128)S(6)} %copy.13.lengths, bf16[128,5120]{1,0:T(8,128)(2,1)S(1)} %bitcast.16, bf16[8,2,128,128]{3,2,1,0:T(8,128)(2,1)} %collective-permute-done.2.refs_0_, ...), custom_call_target="tpu_custom_call" | custom-call | tf_op jit(solution)/shard_map/pallas_call | solution.py:297
  (19 shorter events, 0.0 us)
Async XLA Ops:
  0.0 64.0 %copy-start = (bf16[1,128,5120]{2,1,0:T(8,128)(2,1)S(1)}, bf16[1,128,5120]{2,1,0:T(8,128)(2,1)}, u32[]{:S(2)}) copy-start(bf16[1,128,5120]{2,1,0:T(8,128)(2,1)} %param.8) | copy-start | bytes 3932164
  1.4 59.7 %copy-start.5 = (bf16[8,2,128,128]{3,2,1,0:T(8,128)(2,1)}, bf16[8,2,128,128]{3,2,1,0:T(8,128)(2,1)S(1)}, u32[]{:S(2)}) copy-start(bf16[8,2,128,128]{3,2,1,0:T(8,128)(2,1)S(1)} %get-tuple-element.7.refs_0_) | copy-start | bytes 1572868
  1.4 11.8 %collective-permute-start.7 = (bf16[2,2,128,128]{3,2,1,0:T(8,128)(2,1)S(1)}, bf16[2,2,128,128]{3,2,1,0:T(8,128)(2,1)S(1)}, u32[]{:S(2)}, u32[]{:S(2)}) collective-permute-start(bf16[2,2,128,128]{3,2,1,0:T(8,128)(2,1)S(1)} %get-tuple-element.8), channel_id=1, source_target_pairs={{0,16},{4,20},{8,24},{12,28},{16,0},{20,4},{24,8},{28,12},{1,17},{... | collective-permute-start | bytes 393224 | tf_op jit(solution)/shard_map/ppermute | solution.py:328
  1.8 11.4 %collective-permute-start.8 = (bf16[2,2,128,128]{3,2,1,0:T(8,128)(2,1)S(1)}, bf16[2,2,128,128]{3,2,1,0:T(8,128)(2,1)S(1)}, u32[]{:S(2)}, u32[]{:S(2)}) collective-permute-start(bf16[2,2,128,128]{3,2,1,0:T(8,128)(2,1)S(1)} %get-tuple-element.8), channel_id=1, source_target_pairs={{0,24},{4,28},{8,0},{12,4},{16,8},{20,12},{24,16},{28,20},{1,25},{... | collective-permute-start | bytes 393224 | tf_op jit(solution)/shard_map/ppermute | solution.py:328
  2.3 11.2 %collective-permute-start.6 = (bf16[2,2,128,128]{3,2,1,0:T(8,128)(2,1)S(1)}, bf16[2,2,128,128]{3,2,1,0:T(8,128)(2,1)S(1)}, u32[]{:S(2)}, u32[]{:S(2)}) collective-permute-start(bf16[2,2,128,128]{3,2,1,0:T(8,128)(2,1)S(1)} %get-tuple-element.8), channel_id=1, source_target_pairs={{0,8},{4,12},{8,16},{12,20},{16,24},{20,28},{24,0},{28,4},{1,9},{5... | collective-permute-start | bytes 393224 | tf_op jit(solution)/shard_map/ppermute | solution.py:328
  13.6 60.1 %copy-start.10 = (s32[1,1,8]{2,1,0:T(1,128)S(1)}, s32[1,1,8]{2,1,0:T(1,128)}, u32[]{:S(2)}) copy-start(s32[1,1,8]{2,1,0:T(1,128)} %param.13) | copy-start | bytes 100
  13.6 60.1 %copy-start.12 = (s32[1,1,8]{2,1,0:T(1,128)S(1)}, s32[1,1,8]{2,1,0:T(1,128)}, u32[]{:S(2)}) copy-start(s32[1,1,8]{2,1,0:T(1,128)} %param.14) | copy-start | bytes 100
  13.6 13.9 %collective-permute-start.9 = (bf16[4,2,2,128,128]{4,3,2,1,0:T(8,128)(2,1)S(1)}, bf16[4,2,2,128,128]{4,3,2,1,0:T(8,128)(2,1)S(1)}, u32[]{:S(2)}, u32[]{:S(2)}) collective-permute-start(bf16[4,2,2,128,128]{4,3,2,1,0:T(8,128)(2,1)S(1)} %pad_maximum_fusion.refs_2_), channel_id=1, source_target_pairs={{0,4},{4,0},{8,12},{12,8},{16,20},{20,16},{24,28},{28,24},{1,5},{5... | collective-permute-start | bytes 1572872 | tf_op jit(solution)/shard_map/ppermute | solution.py:328
  15.2 16.9 %collective-permute-start = (bf16[8,2,128,128]{3,2,1,0:T(8,128)(2,1)S(1)}, bf16[8,2,128,128]{3,2,1,0:T(8,128)(2,1)}, u32[]{:S(2)}, u32[]{:S(2)}) collective-permute-start(bf16[8,2,128,128]{3,2,1,0:T(8,128)(2,1)S(1)} %get-tuple-element.7.refs_0_), channel_id=1, source_target_pairs={{0,8},{4,12},{8,16},{12,20},{16,24},{20,28},{1,9},{5,13},{9,17},{1... | collective-permute-start | bytes 1572872 | tf_op jit(solution)/shard_map/ppermute | solution.py:328
  16.5 22.3 %collective-permute-start.16 = (bf16[8,2,128,128]{3,2,1,0:T(8,128)(2,1)S(1)}, bf16[8,2,128,128]{3,2,1,0:T(8,128)(2,1)S(1)}, u32[]{:S(2)}, u32[]{:S(2)}) collective-permute-start(bf16[8,2,128,128]{3,2,1,0:T(8,128)(2,1)S(1)} %get-tuple-element.7.refs_0_), channel_id=1, source_target_pairs={{0,4},{8,12},{16,20},{24,28},{1,5},{9,13},{17,21},{25,29},{2,6},{1... | collective-permute-start | bytes 1572872 | tf_op jit(solution)/shard_map/ppermute | solution.py:328
  18.9 21.9 %collective-permute-start.10 = (bf16[4,2,2,128,128]{4,3,2,1,0:T(8,128)(2,1)S(1)}, bf16[4,2,2,128,128]{4,3,2,1,0:T(8,128)(2,1)S(1)}, u32[]{:S(2)}, u32[]{:S(2)}) collective-permute-start(bf16[4,2,2,128,128]{4,3,2,1,0:T(8,128)(2,1)S(1)} %pad_maximum_fusion.refs_2_), channel_id=1, source_target_pairs={{0,2},{1,3},{2,0},{3,1},{4,6},{5,7},{6,4},{7,5},{8,10},{9,11},{10,... | collective-permute-start | bytes 1572872 | tf_op jit(solution)/shard_map/ppermute | solution.py:328
  19.5 21.4 %collective-permute-start.12 = (bf16[4,2,2,128,128]{4,3,2,1,0:T(8,128)(2,1)S(1)}, bf16[4,2,2,128,128]{4,3,2,1,0:T(8,128)(2,1)S(1)}, u32[]{:S(2)}, u32[]{:S(2)}) collective-permute-start(bf16[4,2,2,128,128]{4,3,2,1,0:T(8,128)(2,1)S(1)} %pad_maximum_fusion.refs_2_), channel_id=1, source_target_pairs={{0,1},{1,0},{2,3},{3,2},{4,5},{5,4},{6,7},{7,6},{8,9},{9,8},{10,11... | collective-permute-start | bytes 1572872 | tf_op jit(solution)/shard_map/ppermute | solution.py:328
  27.5 15.8 %collective-permute-start.11 = (bf16[4,2,2,128,128]{4,3,2,1,0:T(8,128)(2,1)S(1)}, bf16[4,2,2,128,128]{4,3,2,1,0:T(8,128)(2,1)}, u32[]{:S(2)}, u32[]{:S(2)}) collective-permute-start(bf16[4,2,2,128,128]{4,3,2,1,0:T(8,128)(2,1)S(1)} %collective-permute-done.9.refs_3_), channel_id=1, source_target_pairs={{0,2},{1,3},{2,0},{3,1},{4,6},{5,7},{6,4},{7,5},{8,10},{9,11},{10,... | collective-permute-start | bytes 1572872 | tf_op jit(solution)/shard_map/ppermute | solution.py:328
  32.0 16.8 %collective-permute-start.1 = (bf16[8,2,128,128]{3,2,1,0:T(8,128)(2,1)}, bf16[8,2,128,128]{3,2,1,0:T(8,128)(2,1)S(1)}, u32[]{:S(2)}, u32[]{:S(2)}) collective-permute-start(bf16[8,2,128,128]{3,2,1,0:T(8,128)(2,1)} %collective-permute-done.refs_2_), channel_id=1, source_target_pairs={{8,12},{12,8},{16,20},{20,16},{24,28},{28,24},{9,13},{13,9},{17,21... | collective-permute-start | bytes 1572872 | tf_op jit(solution)/shard_map/ppermute | solution.py:328
  38.7 0.8 copy-start.7
  39.6 17.1 %collective-permute-start.3 = (bf16[8,2,128,128]{3,2,1,0:T(8,128)(2,1)}, bf16[8,2,128,128]{3,2,1,0:T(8,128)(2,1)}, u32[]{:S(2)}, u32[]{:S(2)}) collective-permute-start(bf16[8,2,128,128]{3,2,1,0:T(8,128)(2,1)} %collective-permute-done.refs_2_), channel_id=1, source_target_pairs={{8,16},{12,20},{16,24},{20,28},{9,17},{13,21},{17,25},{21,29},{10,... | collective-permute-start | bytes 1572872 | tf_op jit(solution)/shard_map/ppermute | solution.py:328
  40.8 20.2 %collective-permute-start.13 = (bf16[4,2,2,128,128]{4,3,2,1,0:T(8,128)(2,1)S(1)}, bf16[4,2,2,128,128]{4,3,2,1,0:T(8,128)(2,1)S(1)}, u32[]{:S(2)}, u32[]{:S(2)}) collective-permute-start(bf16[4,2,2,128,128]{4,3,2,1,0:T(8,128)(2,1)S(1)} %collective-permute-done.9.refs_3_), channel_id=1, source_target_pairs={{0,1},{1,0},{2,3},{3,2},{4,5},{5,4},{6,7},{7,6},{8,9},{9,8},{10,11... | collective-permute-start | bytes 1572872 | tf_op jit(solution)/shard_map/ppermute | solution.py:328
  40.9 0.8 copy-start.1
  41.7 31.9 %collective-permute-start.14 = (bf16[4,2,2,128,128]{4,3,2,1,0:T(8,128)(2,1)S(1)}, bf16[4,2,2,128,128]{4,3,2,1,0:T(8,128)(2,1)}, u32[]{:S(2)}, u32[]{:S(2)}) collective-permute-start(bf16[4,2,2,128,128]{4,3,2,1,0:T(8,128)(2,1)S(1)} %collective-permute-done.10.refs_4_), channel_id=1, source_target_pairs={{0,1},{1,0},{2,3},{3,2},{4,5},{5,4},{6,7},{7,6},{8,9},{9,8},{10,11... | collective-permute-start | bytes 1572872 | tf_op jit(solution)/shard_map/ppermute | solution.py:328
  43.3 30.3 %collective-permute-start.15 = (bf16[4,2,2,128,128]{4,3,2,1,0:T(8,128)(2,1)}, bf16[4,2,2,128,128]{4,3,2,1,0:T(8,128)(2,1)}, u32[]{:S(2)}, u32[]{:S(2)}) collective-permute-start(bf16[4,2,2,128,128]{4,3,2,1,0:T(8,128)(2,1)} %collective-permute-done.11.refs_5_), channel_id=1, source_target_pairs={{0,1},{1,0},{2,3},{3,2},{4,5},{5,4},{6,7},{7,6},{8,9},{9,8},{10,11... | collective-permute-start | bytes 1572872 | tf_op jit(solution)/shard_map/ppermute | solution.py:328
  48.8 37.3 %collective-permute-start.5 = (bf16[8,2,128,128]{3,2,1,0:T(8,128)(2,1)}, bf16[8,2,128,128]{3,2,1,0:T(8,128)(2,1)}, u32[]{:S(2)}, u32[]{:S(2)}) collective-permute-start(bf16[8,2,128,128]{3,2,1,0:T(8,128)(2,1)} %collective-permute-done.refs_2_), channel_id=1, source_target_pairs={{8,24},{12,28},{9,25},{13,29},{10,26},{14,30},{11,27},{15,31}} | collective-permute-start | bytes 1572872 | tf_op jit(solution)/shard_map/ppermute | solution.py:328
  56.7 29.4 %collective-permute-start.4 = (bf16[8,2,128,128]{3,2,1,0:T(8,128)(2,1)}, bf16[8,2,128,128]{3,2,1,0:T(8,128)(2,1)}, u32[]{:S(2)}, u32[]{:S(2)}) collective-permute-start(bf16[8,2,128,128]{3,2,1,0:T(8,128)(2,1)} %collective-permute-done.3.refs_1_), channel_id=1, source_target_pairs={{16,20},{20,16},{24,28},{28,24},{17,21},{21,17},{25,29},{29,25},{1... | collective-permute-start | bytes 1572872 | tf_op jit(solution)/shard_map/ppermute | solution.py:328
  61.1 0.8 copy-start.3
  61.9 25.7 %collective-permute-start.2 = (bf16[8,2,128,128]{3,2,1,0:T(8,128)(2,1)S(1)}, bf16[8,2,128,128]{3,2,1,0:T(8,128)(2,1)}, u32[]{:S(2)}, u32[]{:S(2)}) collective-permute-start(bf16[8,2,128,128]{3,2,1,0:T(8,128)(2,1)S(1)} %collective-permute-done.1.refs_0_), channel_id=1, source_target_pairs={{8,24},{12,28},{9,25},{13,29},{10,26},{14,30},{11,27},{15,31}} | collective-permute-start | bytes 1572872 | tf_op jit(solution)/shard_map/ppermute | solution.py:328
  63.2 10.5 %copy-start.2 = (bf16[4,2,2,128,128]{4,3,2,1,0:T(8,128)(2,1)S(1)}, bf16[4,2,2,128,128]{4,3,2,1,0:T(8,128)(2,1)}, u32[]{:S(2)}) copy-start(bf16[4,2,2,128,128]{4,3,2,1,0:T(8,128)(2,1)} %copy-done.1) | copy-start | bytes 1572868
  63.2 10.5 %copy-start.4 = (bf16[4,2,2,128,128]{4,3,2,1,0:T(8,128)(2,1)S(1)}, bf16[4,2,2,128,128]{4,3,2,1,0:T(8,128)(2,1)}, u32[]{:S(2)}) copy-start(bf16[4,2,2,128,128]{4,3,2,1,0:T(8,128)(2,1)} %copy-done.3) | copy-start | bytes 1572868
  64.0 1.0 %copy-start.6 = (bf16[8,2,128,128]{3,2,1,0:T(8,128)(2,1)S(1)}, bf16[8,2,128,128]{3,2,1,0:T(8,128)(2,1)}, u32[]{:S(2)}) copy-start(bf16[8,2,128,128]{3,2,1,0:T(8,128)(2,1)} %copy-done.5) | copy-start | bytes 1572868
  65.1 1.0 %copy-start.8 = (bf16[8,2,128,128]{3,2,1,0:T(8,128)(2,1)S(1)}, bf16[8,2,128,128]{3,2,1,0:T(8,128)(2,1)}, u32[]{:S(2)}) copy-start(bf16[8,2,128,128]{3,2,1,0:T(8,128)(2,1)} %copy-done.7) | copy-start | bytes 1572868
  66.1 0.7 copy-start.9
  66.8 0.7 copy-start.11

commit v3 on v2

--- a/solution.py
+++ b/solution.py
@@ -74,32 +74,30 @@
     )
 
 
-def head_of(step, samp_index, shares):
-    per_share = KV_HEADS // shares
-    half = KV_HEADS // 2
-    core_rel = step // half
-    inner = step % half
-    x_rel = inner // per_share
-    share = samp_index ^ (x_rel * 2 + core_rel)
-    return share * per_share + inner % per_share
-
-
 def attend_kernel(plan, place, pre_row, suf_row, lengths, query_ref, *refs):
-    slots, prefix_count, rows, shares, first, last = plan
+    slots, ways, prefix_count, rows, shares, heads, first, last = plan
     refs = list(refs)
-    block_refs = [[refs.pop(0) for _ in range(parts)] for slot, parts in slots]
-    slots = [slot for slot, parts in slots]
-    prefix_refs = [refs.pop(0) for _ in range(8)] if prefix_count else []
+    block_refs = [(refs.pop(0), head_offset) for slot, head_offset in slots]
+    slots = [slot for slot, head_offset in slots]
+    prefix_refs = [(refs.pop(0), refs.pop(0)) for way in ways]
     state_ref = None if first else refs.pop(0)
+    if last and heads[0] > 0:
+        refs.pop(0)
     out_ref = refs.pop(0)
-    if first or not last:
+    if not last:
         state_ref = out_ref
-    key_buffer, value_buffer, seen_list = refs
-    half = KV_HEADS // 2
+    key_buffer, value_buffer, seen_list, out_buffer, out_semaphores = refs
+    turns = heads[1] // TOGETHER
     per_share = KV_HEADS // shares
     seq_index, samp_index = place[0], place[1]
     row, column = seq_index // COLUMNS, seq_index % COLUMNS
     live = seq_index < lengths[0]
+
+    def leave(turn):
+        lanes = pl.ds((heads[0] + turn * TOGETHER) * WIDE, TOGETHER * WIDE)
+        return pltpu.make_async_copy(
+            out_buffer.at[turn], out_ref.at[:, lanes], out_semaphores.at[turn]
+        )
 
     def suffix_seen(slot):
         back, across = slot
@@ -130,13 +128,14 @@
 
             near_count = lax.fori_loop(0, rows, note, jnp.int32(0))
             prefix_seen_count = lax.fori_loop(rows, prefix_count, note, near_count)
-        count = suffix_end + prefix_seen_count
 
         def some_heads(turn, unused):
-            step = turn * TOGETHER
-            head = head_of(step, samp_index, shares)
-            inner = step % half
+            head = heads[0] + turn * TOGETHER
+            relative = (head // per_share) ^ samp_index
+            my_way = relative % 2 * 2 + relative // 2
             lanes = range(TOGETHER)
+            has_prefix = sum((my_way == way).astype(jnp.int32) for way in ways)
+            count = suffix_end + prefix_seen_count * has_prefix
 
             def take(position, sources):
                 for i, source in enumerate(sources):
@@ -144,13 +143,8 @@
                     value_buffer[i, position] = source[1]
 
             def take_block(n, position):
-                parts = block_refs[n]
-                height = KV_HEADS // len(parts)
-                for m, part in enumerate(parts):
-
-                    @pl.when((head >= m * height) & (head < (m + 1) * height))
-                    def _(m=m, part=part):
-                        take(position, [part.at[head - m * height + i] for i in lanes])
+                ref, head_offset = block_refs[n]
+                take(position, [ref.at[head - head_offset + i] for i in lanes])
 
             for n, (seen, position) in enumerate(places):
                 if seen is True:
@@ -158,16 +152,15 @@
                 else:
                     pl.when(seen)(functools.partial(take_block, n, position))
 
-            for way in range(4 if prefix_count else 0):
-                pieces = prefix_refs[way * 2 : way * 2 + 2]
+            for way, pieces in zip(ways, prefix_refs):
 
                 def take_prefix(ref, skipped, n, unused):
                     chosen = ref.at[seen_list[n] - skipped]
-                    first_head = inner % per_share
+                    first_head = head % per_share
                     take(suffix_end + n, [chosen.at[first_head + i] for i in lanes])
                     return unused
 
-                @pl.when(step // per_share == way)
+                @pl.when(my_way == way)
                 def _(pieces=pieces):
                     lax.fori_loop(0, near_count, functools.partial(take_prefix, pieces[0], 0), 0)
                     lax.fori_loop(
@@ -189,7 +182,7 @@
                 )
                 for i in lanes
             ]
-            state = [state_ref.at[step + i] for i in lanes]
+            state = [state_ref.at[head + i] for i in lanes]
             sums = slice(HEAD_DIM + 8, HEAD_DIM + 16)
 
             def chunk(start, size, fresh):
@@ -266,47 +259,64 @@
                     inverse = 1.0 / jnp.sum(state[i][sums], axis=0, keepdims=True)
                     mixed = (state[i][:HEAD_DIM] * inverse).astype(jnp.bfloat16)
                     parts += [mixed[:, j * BLOCK : (j + 1) * BLOCK].T for j in range(GROUP)]
-                out_ref[:, pl.ds(offset, TOGETHER * WIDE)] = jnp.concatenate(parts, axis=1)
+                out_buffer[turn] = jnp.concatenate(parts, axis=1)
+                leave(turn).start()
             return unused
 
-        lax.fori_loop(0, KV_HEADS // TOGETHER, some_heads, 0)
+        lax.fori_loop(0, turns, some_heads, 0)
 
     if last:
 
         @pl.when(jnp.logical_not(live))
         def blank():
-            out_ref[...] = jnp.zeros_like(out_ref)
-
-
-def attend(tables, queries, slots, blocks, prefix, state, shares, rows, last):
+            out_buffer[...] = jnp.zeros_like(out_buffer)
+            for turn in range(turns):
+                leave(turn).start()
+
+        for turn in range(turns):
+            leave(turn).wait()
+
+
+def attend(tables, queries, slots, blocks, prefix, state, out, heads, shares, rows):
+    ways = tuple(prefix)
+    prefix = [piece for way in ways for piece in prefix[way]]
     prefix_count = prefix[0].shape[0] * COLUMNS if prefix else 0
     first = state is None
+    last = heads != (0, KV_HEADS)
     total = len(slots) + prefix_count
-    plan = tuple((slot, len(parts)) for slot, parts in zip(slots, blocks))
-    blocks = [part for parts in blocks for part in parts]
-    state_shape = (KV_HEADS, HEAD_DIM + 16, WIDE)
+    plan = tuple((slot, head_offset) for slot, (block, head_offset) in zip(slots, blocks))
+    inside = pl.BlockSpec(memory_space=pltpu.VMEM)
+    outside = pl.BlockSpec(memory_space=pltpu.HBM)
+    table = pl.BlockSpec(memory_space=pltpu.SMEM)
+    operands = [queries, *(block for block, head_offset in blocks), *prefix]
+    operands += [] if first else [state]
+    operands = [pltpu.with_memory_space_constraint(x, pltpu.VMEM) for x in operands]
+    in_specs = [table] * len(tables) + [inside] * len(operands)
     if last:
-        out_shape = jax.ShapeDtypeStruct((BLOCK, HEADS * HEAD_DIM), jnp.bfloat16)
+        out_shape = pltpu.HBM((BLOCK, HEADS * HEAD_DIM), jnp.bfloat16)
+        if out is not None:
+            operands.append(pltpu.with_memory_space_constraint(out, pltpu.HBM))
+            in_specs.append(outside)
     else:
-        out_shape = pltpu.VMEM(state_shape, jnp.float32)
-    operands = [queries, *blocks, *prefix] + ([] if first else [state])
-    operands = [pltpu.with_memory_space_constraint(x, pltpu.VMEM) for x in operands]
-    inside = pl.BlockSpec(memory_space=pltpu.VMEM)
-    table = pl.BlockSpec(memory_space=pltpu.SMEM)
-    aliases = {} if first or last else {len(tables) + len(operands) - 1: 0}
+        out_shape = pltpu.VMEM((KV_HEADS, HEAD_DIM + 16, WIDE), jnp.float32)
+    aliased = out is not None or not (first or last)
+    turns = heads[1] // TOGETHER if last else 1
+    buffer_width = TOGETHER * WIDE if last else HEAD_DIM
     return pl.pallas_call(
         functools.partial(
-            attend_kernel, (plan, prefix_count, rows, shares, first, last)
+            attend_kernel, (plan, ways, prefix_count, rows, shares, heads, first, last)
         ),
         out_shape=out_shape,
-        in_specs=[table] * len(tables) + [inside] * len(operands),
-        out_specs=inside,
+        in_specs=in_specs,
+        out_specs=outside if last else inside,
         scratch_shapes=[
             pltpu.VMEM((TOGETHER, total, BLOCK, HEAD_DIM), jnp.bfloat16),
             pltpu.VMEM((TOGETHER, total, HEAD_DIM, BLOCK), jnp.bfloat16),
             pltpu.SMEM((max(prefix_count, 1) + 1,), jnp.int32),
+            pltpu.VMEM((turns, BLOCK, buffer_width), jnp.bfloat16),
+            pltpu.SemaphoreType.DMA((turns,)),
         ],
-        input_output_aliases=aliases,
+        input_output_aliases={len(in_specs) - 1: 0} if aliased else {},
         compiler_params=pltpu.CompilerParams(vmem_limit_bytes=10 * 2**20 + total * 2**17),
     )(*tables, *operands)
 
@@ -335,6 +345,7 @@
 
     held = {(0, False): own}
     top = rows - 1
+    low, high = slice(0, KV_HEADS // 2), slice(KV_HEADS // 2, KV_HEADS)
     across = [(z * COLUMNS, z * COLUMNS + 1) for z in range(rows)]
     held[0, True] = move(own, across)
     for k in range(1, rows):
@@ -343,8 +354,11 @@
             held[k, False] = move(held[k - 1, False], upward)
             held[k, True] = move(held[k, False], swap_columns[k * COLUMNS :])
         else:
-            held[k, False] = move(held[1, False], along_rows([(1, top)]))
-            held[k, True] = move(held[1, True], along_rows([(1, top)]))
+            from_row = along_rows([(1, top)])
+            straight = move(held[1, False][low], from_row)
+            relayed = move(held[k - 1, False][high], along_rows([(top - 1, top)]))
+            held[k, False] = (straight, relayed)
+            held[k, True] = tuple(move(held[1, True][part], from_row) for part in (low, high))
 
     gathered = [own_share]
     for k in range(1, rows):
@@ -358,9 +372,11 @@
     other_x = move(other, swap_x, "samp")
     near = [same, other, same_x, other_x]
     far = [move(piece, swap_core, "samp") for piece in near]
-
-    early, late, latest = stages(rows)
-    middle = [slot for slot in held if slot not in early + late + latest]
+    straight_ways = {0: near[:2], 2: far[:2]}
+    crossed_ways = {1: near[2:], 3: far[2:]}
+
+    groups = stages(rows)
+    groups[2] = [slot for slot in held if slot not in sum(groups, [])]
     tables = (
         jnp.stack([seq_index, samp_index]).astype(jnp.int32),
         layout_pre[0, 0],
@@ -368,22 +384,28 @@
         lengths,
     )
 
-    def run(slots, prefix, state, last):
-        blocks = [held[slot] if isinstance(held[slot], tuple) else (held[slot],) for slot in slots]
-        return attend(tables, queries[0], slots, blocks, prefix, state, shares, rows, last)
-
-    state = run(early, [], None, False)
-    state = run(middle, near + far, state, False)
-    if late:
-        state = run(late, [], state, False)
-    return run(latest, [], state, True)[None]
+    def run(slots, prefix, state, out, heads):
+        blocks = []
+        for slot in slots:
+            split = isinstance(held[slot], tuple)
+            blocks.append((held[slot][heads[0] > 0], heads[0]) if split else (held[slot], 0))
+        return attend(tables, queries[0], slots, blocks, prefix, state, out, heads, shares, rows)
+
+    state = None
+    for n, prefix in enumerate([{}, straight_ways, crossed_ways]):
+        state = run(groups[n], prefix, state, None, (0, KV_HEADS))
+    half = KV_HEADS // 2
+    out = run(groups[3], {}, state, None, (0, half))
+    return run(groups[3], {}, state, out, (half, half))[None]
 
 
 def stages(rows):
-    early = [(0, False), (0, True)] + [(1, False)] * (rows > 2)
-    late = [(rows - 2, True), (rows - 1, False)] if rows > 2 else []
-    latest = [(rows - 1, True)] + [(rows - 1, False)] * (rows <= 2)
-    return early, late, latest
+    return [
+        [(0, False), (0, True)],
+        [(1, False)],
+        [],
+        [(rows - 2, True), (rows - 1, False), (rows - 1, True)],
+    ]
 
 
 def solution(mesh):

time: 93 us -> 92.1 us (level)
  waiting for transfers between devices: 37.3 us -> 28.3 us
  starting transfers between devices: 21.9 us -> 26.7 us
  local copies, waits for them, and re-layouts: 5.82 us -> 9.22 us
    ppermute x17 -> x19, waiting for transfers between devices: 37.3 us -> 28.3 us  [move(): return lax.ppermute(value, axis, pairs)]
    ppermute x17 -> x19, starting transfers between devices: 21.9 us -> 26.7 us  [move(): return lax.ppermute(value, axis, pairs)]
    slice x0 -> x3, local copies, waits for them, and re-layouts: none -> 2.29 us  [the longest x1 0.84 us: shards(): held[1, True][part]]
    unnamed x26 -> x46, local copies, waits for them, and re-layouts: 5.82 us -> 6.93 us
    pallas_call x4 -> x5, Pallas kernels: 25 us -> 24.8 us  [attend(): pl.pallas_call(functools.partial(attend_kernel, (plan, ways, prefix_count...]
  transfers between devices with their start and end apart: 17 -> 19, of which waited for: 8 -> 8; matrix products, arithmetic and copies ran while one was open for 0% -> 3% of each run, Pallas kernels for 22% -> 23%
where the time goes in v3:
time: 92.1 us; the launch traced here: 91.7 us
  waiting for transfers between devices  28.3 us (31%)
  starting transfers between devices  26.7 us (29%)
  Pallas kernels  26.2 us (28%)
  local copies, waits for them, and re-layouts  9.22 us (10%)
  between operations  1.08 us (1%)
    ppermute x19, waiting for transfers between devices, move(): return lax.ppermute(value, axis, pairs)  28.3 us
    ppermute x19, starting transfers between devices, move(): return lax.ppermute(value, axis, pairs)  26.7 us
    pallas_call x5, Pallas kernels, attend(): pl.pallas_call(functools.partial(attend_kernel, (plan, ways, prefix_count...  24.8 us
    unnamed x46, local copies, waits for them, and re-layouts  6.93 us
  transfers between devices with their start and end apart: 19, of which 8 were waited for; matrix products, arithmetic and copies ran while one was open for 3% of the time, Pallas kernels for 23%

profile of v3, /device:TPU:26, one launch (start us, length us, event | category | flops | bytes accessed | tf_op | source)
XLA Modules:
  0.0 91.7 jit_solution(17580081905307282391)
XLA Ops:
  0.0 1.4 %pack.1 = (bf16[8,2,128,128]{3,2,1,0:T(8,128)(2,1)S(1)}, bf16[2,2,128,128]{3,2,1,0:T(8,128)(2,1)S(1)}) custom-call(s32[1]{0:T(128)} %bitcast.5.first_ref, bf16[128,1024]{1,0:T(8,128)(2,1)} %refs_0_.1, bf16[128,1024]{1,0:T(8,128)(2,1)} %refs_1_.1, bf16[128,1024]{1,0:T(8,128)(2,1)} %bitcast.29, bf16[128,1024]{1,0:T(8,128)(2,1)} %bitcast.30), custom_call_target="tpu_custom_call" | custom-call | tf_op jit(solution)/shard_map/pack/pallas_call | solution.py:52
  1.4 0.4 collective-permute-start.7
  1.8 0.4 collective-permute-start.8
  2.3 3.4 %collective-permute-start.6 = (bf16[2,2,128,128]{3,2,1,0:T(8,128)(2,1)S(1)}, bf16[2,2,128,128]{3,2,1,0:T(8,128)(2,1)S(1)}, u32[]{:S(2)}, u32[]{:S(2)}) collective-permute-start(bf16[2,2,128,128]{3,2,1,0:T(8,128)(2,1)S(1)} %get-tuple-element.8), channel_id=1, source_target_pairs={{0,8},{4,12},{8,16},{12,20},{16,24},{20,28},{24,0},{28,4},{1,9},{5... | collective-permute-start | bytes 393224 | tf_op jit(solution)/shard_map/ppermute | solution.py:338
  5.7 1.3 %collective-permute-start = (bf16[8,2,128,128]{3,2,1,0:T(8,128)(2,1)S(1)}, bf16[8,2,128,128]{3,2,1,0:T(8,128)(2,1)S(1)}, u32[]{:S(2)}, u32[]{:S(2)}) collective-permute-start(bf16[8,2,128,128]{3,2,1,0:T(8,128)(2,1)S(1)} %get-tuple-element.7.refs_0_), channel_id=1, source_target_pairs={{0,8},{4,12},{8,16},{12,20},{16,24},{20,28},{1,9},{5,13},{9,17},{1... | collective-permute-start | bytes 1572872 | tf_op jit(solution)/shard_map/ppermute | solution.py:338
  7.0 6.3 %collective-permute-done.7 = bf16[2,2,128,128]{3,2,1,0:T(8,128)(2,1)S(1)} collective-permute-done((bf16[2,2,128,128]{3,2,1,0:T(8,128)(2,1)S(1)}, bf16[2,2,128,128]{3,2,1,0:T(8,128)(2,1)S(1)}, u32[]{:S(2)}, u32[]{:S(2)}) %collective-permute-start.7) | collective-permute-done | bytes 131104 | tf_op jit(solution)/shard_map/ppermute | solution.py:338
  13.3 0.0 collective-permute-done.8
  13.3 0.5 collective-permute-done.6
  13.8 0.1 pad_maximum_fusion.refs_1_
  13.9 1.6 %collective-permute-start.10 = (bf16[4,2,2,128,128]{4,3,2,1,0:T(8,128)(2,1)S(1)}, bf16[4,2,2,128,128]{4,3,2,1,0:T(8,128)(2,1)S(1)}, u32[]{:S(2)}, u32[]{:S(2)}) collective-permute-start(bf16[4,2,2,128,128]{4,3,2,1,0:T(8,128)(2,1)S(1)} %pad_maximum_fusion.refs_1_), channel_id=1, source_target_pairs={{0,4},{4,0},{8,12},{12,8},{16,20},{20,16},{24,28},{28,24},{1,5},{5... | collective-permute-start | bytes 1572872 | tf_op jit(solution)/shard_map/ppermute | solution.py:338
  15.4 2.4 %collective-permute-start.16 = (bf16[8,2,128,128]{3,2,1,0:T(8,128)(2,1)S(1)}, bf16[8,2,128,128]{3,2,1,0:T(8,128)(2,1)S(1)}, u32[]{:S(2)}, u32[]{:S(2)}) collective-permute-start(bf16[8,2,128,128]{3,2,1,0:T(8,128)(2,1)S(1)} %get-tuple-element.7.refs_0_), channel_id=1, source_target_pairs={{0,4},{8,12},{16,20},{24,28},{1,5},{9,13},{17,21},{25,29},{2,6},{1... | collective-permute-start | bytes 1572872 | tf_op jit(solution)/shard_map/ppermute | solution.py:338
  17.9 0.6 collective-permute-start.9
  18.5 6.3 %collective-permute-done.refs_0_ = bf16[8,2,128,128]{3,2,1,0:T(8,128)(2,1)S(1)} collective-permute-done((bf16[8,2,128,128]{3,2,1,0:T(8,128)(2,1)S(1)}, bf16[8,2,128,128]{3,2,1,0:T(8,128)(2,1)S(1)}, u32[]{:S(2)}, u32[]{:S(2)}) %collective-permute-start) | collective-permute-done | bytes 524320 | tf_op jit(solution)/shard_map/ppermute | solution.py:338
  24.8 1.3 %collective-permute-start.1 = (bf16[8,2,128,128]{3,2,1,0:T(8,128)(2,1)S(1)}, bf16[8,2,128,128]{3,2,1,0:T(8,128)(2,1)S(1)}, u32[]{:S(2)}, u32[]{:S(2)}) collective-permute-start(bf16[8,2,128,128]{3,2,1,0:T(8,128)(2,1)S(1)} %collective-permute-done.refs_0_), channel_id=1, source_target_pairs={{8,16},{12,20},{16,24},{20,28},{9,17},{13,21},{17,25},{21,29},{10,... | collective-permute-start | bytes 1572872 | tf_op jit(solution)/shard_map/ppermute | solution.py:338
  26.0 1.7 %collective-permute-done.10.refs_2_ = bf16[4,2,2,128,128]{4,3,2,1,0:T(8,128)(2,1)S(1)} collective-permute-done((bf16[4,2,2,128,128]{4,3,2,1,0:T(8,128)(2,1)S(1)}, bf16[4,2,2,128,128]{4,3,2,1,0:T(8,128)(2,1)S(1)}, u32[]{:S(2)}, u32[]{:S(2)}) %collective-permute-start.10) | collective-permute-done | bytes 524320 | tf_op jit(solution)/shard_map/ppermute | solution.py:338
  27.8 0.5 collective-permute-start.11
  28.3 4.4 %collective-permute-start.4 = (bf16[8,2,128,128]{3,2,1,0:T(8,128)(2,1)S(1)}, bf16[8,2,128,128]{3,2,1,0:T(8,128)(2,1)S(1)}, u32[]{:S(2)}, u32[]{:S(2)}) collective-permute-start(bf16[8,2,128,128]{3,2,1,0:T(8,128)(2,1)S(1)} %collective-permute-done.refs_0_), channel_id=1, source_target_pairs={{8,12},{12,8},{16,20},{20,16},{24,28},{28,24},{9,13},{13,9},{17,21... | collective-permute-start | bytes 1572872 | tf_op jit(solution)/shard_map/ppermute | solution.py:338
  32.7 6.3 %collective-permute-done.16.refs_1_ = bf16[8,2,128,128]{3,2,1,0:T(8,128)(2,1)S(1)} collective-permute-done((bf16[8,2,128,128]{3,2,1,0:T(8,128)(2,1)S(1)}, bf16[8,2,128,128]{3,2,1,0:T(8,128)(2,1)S(1)}, u32[]{:S(2)}, u32[]{:S(2)}) %collective-permute-start.16) | collective-permute-done | bytes 524320 | tf_op jit(solution)/shard_map/ppermute | solution.py:338
  39.0 0.8 copy-done.7
  39.8 0.0 collective-permute-start.14
  39.8 0.0 collective-permute-done.9.refs_2_
  39.8 0.5 collective-permute-start.15
  40.3 0.8 copy-done.15
  41.1 0.7 collective-permute-done.1.refs_1_
  41.8 0.1 collective-permute-done.11.refs_3_
  41.9 0.4 collective-permute-start.13
  42.3 6.4 %collective-permute-done.4.refs_0_ = bf16[8,2,128,128]{3,2,1,0:T(8,128)(2,1)S(1)} collective-permute-done((bf16[8,2,128,128]{3,2,1,0:T(8,128)(2,1)S(1)}, bf16[8,2,128,128]{3,2,1,0:T(8,128)(2,1)S(1)}, u32[]{:S(2)}, u32[]{:S(2)}) %collective-permute-start.4) | collective-permute-done | bytes 524320 | tf_op jit(solution)/shard_map/ppermute | solution.py:338
  48.7 4.4 %collective-permute-start.2 = (bf16[8,2,128,128]{3,2,1,0:T(8,128)(2,1)S(1)}, bf16[8,2,128,128]{3,2,1,0:T(8,128)(2,1)S(1)}, u32[]{:S(2)}, u32[]{:S(2)}) collective-permute-start(bf16[8,2,128,128]{3,2,1,0:T(8,128)(2,1)S(1)} %collective-permute-done.1.refs_1_), channel_id=1, source_target_pairs={{16,20},{20,16},{24,28},{28,24},{17,21},{21,17},{25,29},{29,25},{1... | collective-permute-start | bytes 1572872 | tf_op jit(solution)/shard_map/ppermute | solution.py:338
  53.1 0.7 slice.18
  53.8 0.7 slice.16
  54.5 0.8 fusion
  55.4 0.8 copy-done.17
  56.2 1.3 %collective-permute-start.17 = (bf16[4,2,128,128]{3,2,1,0:T(8,128)(2,1)}, bf16[4,2,128,128]{3,2,1,0:T(8,128)(2,1)}, u32[]{:S(2)}, u32[]{:S(2)}) collective-permute-start(bf16[4,2,128,128]{3,2,1,0:T(8,128)(2,1)} %slice.18), channel_id=1, source_target_pairs={{8,24},{12,28},{9,25},{13,29},{10,26},{14,30},{11,27},{15,31}} | collective-permute-start | bytes 786440 | tf_op jit(solution)/shard_map/ppermute | solution.py:338
  57.5 0.8 copy-done.19
  58.3 1.3 %collective-permute-start.18 = (bf16[4,2,128,128]{3,2,1,0:T(8,128)(2,1)}, bf16[4,2,128,128]{3,2,1,0:T(8,128)(2,1)}, u32[]{:S(2)}, u32[]{:S(2)}) collective-permute-start(bf16[4,2,128,128]{3,2,1,0:T(8,128)(2,1)} %get-tuple-element.9), channel_id=1, source_target_pairs={{8,24},{12,28},{9,25},{13,29},{10,26},{14,30},{11,27},{15,31}} | collective-permute-start | bytes 786440 | tf_op jit(solution)/shard_map/ppermute | solution.py:338
  59.6 0.8 copy-done.11
  60.4 1.3 %collective-permute-start.5 = (bf16[4,2,128,128]{3,2,1,0:T(8,128)(2,1)}, bf16[4,2,128,128]{3,2,1,0:T(8,128)(2,1)}, u32[]{:S(2)}, u32[]{:S(2)}) collective-permute-start(bf16[4,2,128,128]{3,2,1,0:T(8,128)(2,1)} %get-tuple-element.10), channel_id=1, source_target_pairs={{8,24},{12,28},{9,25},{13,29},{10,26},{14,30},{11,27},{15,31}} | collective-permute-start | bytes 786440 | tf_op jit(solution)/shard_map/ppermute | solution.py:338
  61.7 0.8 copy-done.13
  62.5 1.3 %collective-permute-start.3 = (bf16[4,2,128,128]{3,2,1,0:T(8,128)(2,1)}, bf16[4,2,128,128]{3,2,1,0:T(8,128)(2,1)}, u32[]{:S(2)}, u32[]{:S(2)}) collective-permute-start(bf16[4,2,128,128]{3,2,1,0:T(8,128)(2,1)} %slice.16), channel_id=1, source_target_pairs={{16,24},{20,28},{17,25},{21,29},{18,26},{22,30},{19,27},{23,31}} | collective-permute-start | bytes 786440 | tf_op jit(solution)/shard_map/ppermute | solution.py:338
  64.5 0.1 pad_add_fusion.place
  64.6 1.0 %copy-done.4 = bf16[8,2,128,128]{3,2,1,0:T(8,128)(2,1)S(1)} copy-done((bf16[8,2,128,128]{3,2,1,0:T(8,128)(2,1)S(1)}, bf16[8,2,128,128]{3,2,1,0:T(8,128)(2,1)}, u32[]{:S(2)}) %copy-start.4) | copy-done | bytes 524312
  65.6 1.0 %copy-done.8 = bf16[8,2,128,128]{3,2,1,0:T(8,128)(2,1)S(1)} copy-done((bf16[8,2,128,128]{3,2,1,0:T(8,128)(2,1)S(1)}, bf16[8,2,128,128]{3,2,1,0:T(8,128)(2,1)}, u32[]{:S(2)}) %copy-start.8) | copy-done | bytes 524312
  66.7 3.5 %shard_map.82.refs_5_ = f32[8,144,640]{2,1,0:T(8,128)S(1)} custom-call(s32[2]{0:T(128)S(1)} %pad_add_fusion.place, s32[8]{0:T(128)S(1)} %bitcast.19, s32[8]{0:T(128)S(1)} %bitcast.24, s32[1]{0:T(128)S(6)} %copy.15.lengths, bf16[128,5120]{1,0:T(8,128)(2,1)S(1)} %bitcast.13, bf16[8,2,128,128]{3,2,1,0:T(8,128)(2,1)S(1)} %copy-done.4, ...), custom_call_target="tpu_custom_call" | custom-call | tf_op jit(solution)/shard_map/pallas_call | solution.py:305
  70.2 0.0 copy-start.6
  70.3 7.2 %shard_map.83.refs_6_ = f32[8,144,640]{2,1,0:T(8,128)S(1)} custom-call(s32[2]{0:T(128)S(1)} %pad_add_fusion.place, s32[8]{0:T(128)S(1)} %bitcast.20, s32[8]{0:T(128)S(1)} %bitcast.25, s32[1]{0:T(128)S(6)} %copy.15.lengths, bf16[128,5120]{1,0:T(8,128)(2,1)S(1)} %bitcast.14, bf16[8,2,128,128]{3,2,1,0:T(8,128)(2,1)S(1)} %copy-done.2, ...), custom_call_target="tpu_custom_call", output_to_operand_aliasing={{}: (10, {})} | custom-call | tf_op jit(solution)/shard_map/pallas_call | solution.py:305
  77.5 7.6 %shard_map.84.refs_3_ = f32[8,144,640]{2,1,0:T(8,128)S(1)} custom-call(s32[2]{0:T(128)S(1)} %pad_add_fusion.place, s32[8]{0:T(128)S(1)} %bitcast.21, s32[8]{0:T(128)S(1)} %bitcast.26, s32[1]{0:T(128)S(6)} %copy.15.lengths, bf16[128,5120]{1,0:T(8,128)(2,1)S(1)} %bitcast.15, ...), custom_call_target="tpu_custom_call", output_to_operand_aliasing={{}: (11, {})} | custom-call | tf_op jit(solution)/shard_map/pallas_call | solution.py:305
  85.1 3.3 %shard_map.85.refs_4_ = bf16[128,5120]{1,0:T(8,128)(2,1)} custom-call(s32[2]{0:T(128)S(1)} %pad_add_fusion.place, s32[8]{0:T(128)S(1)} %bitcast.22, s32[8]{0:T(128)S(1)} %bitcast.27, s32[1]{0:T(128)S(6)} %copy.15.lengths, bf16[128,5120]{1,0:T(8,128)(2,1)S(1)} %bitcast.16, bf16[8,2,128,128]{3,2,1,0:T(8,128)(2,1)S(1)} %collective-permute-done.2.refs_0_, ...), custom_call_target="tpu_custom_call" | custom-call | tf_op jit(solution)/shard_map/pallas_call | solution.py:305
  88.4 3.3 %shard_map.86 = bf16[128,5120]{1,0:T(8,128)(2,1)} custom-call(s32[2]{0:T(128)S(1)} %pad_add_fusion.place, s32[8]{0:T(128)S(1)} %bitcast.23, s32[8]{0:T(128)S(1)} %bitcast.28, s32[1]{0:T(128)S(6)} %copy.15.lengths, bf16[128,5120]{1,0:T(8,128)(2,1)S(1)} %bitcast.17, ...), custom_call_target="tpu_custom_call", output_to_operand_aliasing={{}: (9, {})} | custom-call | tf_op jit(solution)/shard_map/pallas_call | solution.py:305
  (47 shorter events, 0.1 us)
Async XLA Ops:
  0.0 64.6 %copy-start.21 = (s32[1,1,8]{2,1,0:T(1,128)S(1)}, s32[1,1,8]{2,1,0:T(1,128)}, u32[]{:S(2)}) copy-start(s32[1,1,8]{2,1,0:T(1,128)} %param.13) | copy-start | bytes 100
  0.0 64.6 %copy-start.22 = (s32[1,1,8]{2,1,0:T(1,128)S(1)}, s32[1,1,8]{2,1,0:T(1,128)}, u32[]{:S(2)}) copy-start(s32[1,1,8]{2,1,0:T(1,128)} %param.14) | copy-start | bytes 100
  0.0 64.6 %copy-start = (bf16[1,128,5120]{2,1,0:T(8,128)(2,1)S(1)}, bf16[1,128,5120]{2,1,0:T(8,128)(2,1)}, u32[]{:S(2)}) copy-start(bf16[1,128,5120]{2,1,0:T(8,128)(2,1)} %param.8) | copy-start | bytes 3932164
  1.4 40.9 %copy-start.3 = (bf16[8,2,128,128]{3,2,1,0:T(8,128)(2,1)}, bf16[8,2,128,128]{3,2,1,0:T(8,128)(2,1)S(1)}, u32[]{:S(2)}) copy-start(bf16[8,2,128,128]{3,2,1,0:T(8,128)(2,1)S(1)} %get-tuple-element.7.refs_0_) | copy-start | bytes 1572868
  1.4 11.8 %collective-permute-start.7 = (bf16[2,2,128,128]{3,2,1,0:T(8,128)(2,1)S(1)}, bf16[2,2,128,128]{3,2,1,0:T(8,128)(2,1)S(1)}, u32[]{:S(2)}, u32[]{:S(2)}) collective-permute-start(bf16[2,2,128,128]{3,2,1,0:T(8,128)(2,1)S(1)} %get-tuple-element.8), channel_id=1, source_target_pairs={{0,16},{4,20},{8,24},{12,28},{16,0},{20,4},{24,8},{28,12},{1,17},{... | collective-permute-start | bytes 393224 | tf_op jit(solution)/shard_map/ppermute | solution.py:338
  1.8 11.4 %collective-permute-start.8 = (bf16[2,2,128,128]{3,2,1,0:T(8,128)(2,1)S(1)}, bf16[2,2,128,128]{3,2,1,0:T(8,128)(2,1)S(1)}, u32[]{:S(2)}, u32[]{:S(2)}) collective-permute-start(bf16[2,2,128,128]{3,2,1,0:T(8,128)(2,1)S(1)} %get-tuple-element.8), channel_id=1, source_target_pairs={{0,24},{4,28},{8,0},{12,4},{16,8},{20,12},{24,16},{28,20},{1,25},{... | collective-permute-start | bytes 393224 | tf_op jit(solution)/shard_map/ppermute | solution.py:338
  2.3 11.5 %collective-permute-start.6 = (bf16[2,2,128,128]{3,2,1,0:T(8,128)(2,1)S(1)}, bf16[2,2,128,128]{3,2,1,0:T(8,128)(2,1)S(1)}, u32[]{:S(2)}, u32[]{:S(2)}) collective-permute-start(bf16[2,2,128,128]{3,2,1,0:T(8,128)(2,1)S(1)} %get-tuple-element.8), channel_id=1, source_target_pairs={{0,8},{4,12},{8,16},{12,20},{16,24},{20,28},{24,0},{28,4},{1,9},{5... | collective-permute-start | bytes 393224 | tf_op jit(solution)/shard_map/ppermute | solution.py:338
  5.7 19.1 %collective-permute-start = (bf16[8,2,128,128]{3,2,1,0:T(8,128)(2,1)S(1)}, bf16[8,2,128,128]{3,2,1,0:T(8,128)(2,1)S(1)}, u32[]{:S(2)}, u32[]{:S(2)}) collective-permute-start(bf16[8,2,128,128]{3,2,1,0:T(8,128)(2,1)S(1)} %get-tuple-element.7.refs_0_), channel_id=1, source_target_pairs={{0,8},{4,12},{8,16},{12,20},{16,24},{20,28},{1,9},{5,13},{9,17},{1... | collective-permute-start | bytes 1572872 | tf_op jit(solution)/shard_map/ppermute | solution.py:338
  13.9 13.9 %collective-permute-start.10 = (bf16[4,2,2,128,128]{4,3,2,1,0:T(8,128)(2,1)S(1)}, bf16[4,2,2,128,128]{4,3,2,1,0:T(8,128)(2,1)S(1)}, u32[]{:S(2)}, u32[]{:S(2)}) collective-permute-start(bf16[4,2,2,128,128]{4,3,2,1,0:T(8,128)(2,1)S(1)} %pad_maximum_fusion.refs_1_), channel_id=1, source_target_pairs={{0,4},{4,0},{8,12},{12,8},{16,20},{20,16},{24,28},{28,24},{1,5},{5... | collective-permute-start | bytes 1572872 | tf_op jit(solution)/shard_map/ppermute | solution.py:338
  15.4 23.6 %collective-permute-start.16 = (bf16[8,2,128,128]{3,2,1,0:T(8,128)(2,1)S(1)}, bf16[8,2,128,128]{3,2,1,0:T(8,128)(2,1)S(1)}, u32[]{:S(2)}, u32[]{:S(2)}) collective-permute-start(bf16[8,2,128,128]{3,2,1,0:T(8,128)(2,1)S(1)} %get-tuple-element.7.refs_0_), channel_id=1, source_target_pairs={{0,4},{8,12},{16,20},{24,28},{1,5},{9,13},{17,21},{25,29},{2,6},{1... | collective-permute-start | bytes 1572872 | tf_op jit(solution)/shard_map/ppermute | solution.py:338
  17.9 21.9 %collective-permute-start.9 = (bf16[4,2,2,128,128]{4,3,2,1,0:T(8,128)(2,1)S(1)}, bf16[4,2,2,128,128]{4,3,2,1,0:T(8,128)(2,1)S(1)}, u32[]{:S(2)}, u32[]{:S(2)}) collective-permute-start(bf16[4,2,2,128,128]{4,3,2,1,0:T(8,128)(2,1)S(1)} %pad_maximum_fusion.refs_1_), channel_id=1, source_target_pairs={{0,2},{1,3},{2,0},{3,1},{4,6},{5,7},{6,4},{7,5},{8,10},{9,11},{10,... | collective-permute-start | bytes 1572872 | tf_op jit(solution)/shard_map/ppermute | solution.py:338
  24.8 30.6 %copy-start.1 = (bf16[8,2,128,128]{3,2,1,0:T(8,128)(2,1)}, bf16[8,2,128,128]{3,2,1,0:T(8,128)(2,1)S(1)}, u32[]{:S(2)}) copy-start(bf16[8,2,128,128]{3,2,1,0:T(8,128)(2,1)S(1)} %collective-permute-done.refs_0_) | copy-start | bytes 1572868
  24.8 17.0 %collective-permute-start.1 = (bf16[8,2,128,128]{3,2,1,0:T(8,128)(2,1)S(1)}, bf16[8,2,128,128]{3,2,1,0:T(8,128)(2,1)S(1)}, u32[]{:S(2)}, u32[]{:S(2)}) collective-permute-start(bf16[8,2,128,128]{3,2,1,0:T(8,128)(2,1)S(1)} %collective-permute-done.refs_0_), channel_id=1, source_target_pairs={{8,16},{12,20},{16,24},{20,28},{9,17},{13,21},{17,25},{21,29},{10,... | collective-permute-start | bytes 1572872 | tf_op jit(solution)/shard_map/ppermute | solution.py:338
  27.8 14.1 %collective-permute-start.11 = (bf16[4,2,2,128,128]{4,3,2,1,0:T(8,128)(2,1)S(1)}, bf16[4,2,2,128,128]{4,3,2,1,0:T(8,128)(2,1)S(1)}, u32[]{:S(2)}, u32[]{:S(2)}) collective-permute-start(bf16[4,2,2,128,128]{4,3,2,1,0:T(8,128)(2,1)S(1)} %collective-permute-done.10.refs_2_), channel_id=1, source_target_pairs={{0,2},{1,3},{2,0},{3,1},{4,6},{5,7},{6,4},{7,5},{8,10},{9,11},{10,... | collective-permute-start | bytes 1572872 | tf_op jit(solution)/shard_map/ppermute | solution.py:338
  28.3 20.4 %collective-permute-start.4 = (bf16[8,2,128,128]{3,2,1,0:T(8,128)(2,1)S(1)}, bf16[8,2,128,128]{3,2,1,0:T(8,128)(2,1)S(1)}, u32[]{:S(2)}, u32[]{:S(2)}) collective-permute-start(bf16[8,2,128,128]{3,2,1,0:T(8,128)(2,1)S(1)} %collective-permute-done.refs_0_), channel_id=1, source_target_pairs={{8,12},{12,8},{16,20},{20,16},{24,28},{28,24},{9,13},{13,9},{17,21... | collective-permute-start | bytes 1572872 | tf_op jit(solution)/shard_map/ppermute | solution.py:338
  39.0 0.8 copy-start.7
  39.8 15.6 %collective-permute-start.14 = (bf16[4,2,2,128,128]{4,3,2,1,0:T(8,128)(2,1)S(1)}, bf16[4,2,2,128,128]{4,3,2,1,0:T(8,128)(2,1)S(1)}, u32[]{:S(2)}, u32[]{:S(2)}) collective-permute-start(bf16[4,2,2,128,128]{4,3,2,1,0:T(8,128)(2,1)S(1)} %pad_maximum_fusion.refs_1_), channel_id=1, source_target_pairs={{0,1},{1,0},{2,3},{3,2},{4,5},{5,4},{6,7},{7,6},{8,9},{9,8},{10,11... | collective-permute-start | bytes 1572872 | tf_op jit(solution)/shard_map/ppermute | solution.py:338
  39.8 17.7 %copy-start.5 = (bf16[4,2,2,128,128]{4,3,2,1,0:T(8,128)(2,1)}, bf16[4,2,2,128,128]{4,3,2,1,0:T(8,128)(2,1)S(1)}, u32[]{:S(2)}) copy-start(bf16[4,2,2,128,128]{4,3,2,1,0:T(8,128)(2,1)S(1)} %collective-permute-done.9.refs_2_) | copy-start | bytes 1572868
  39.8 17.7 %collective-permute-start.15 = (bf16[4,2,2,128,128]{4,3,2,1,0:T(8,128)(2,1)S(1)}, bf16[4,2,2,128,128]{4,3,2,1,0:T(8,128)(2,1)S(1)}, u32[]{:S(2)}, u32[]{:S(2)}) collective-permute-start(bf16[4,2,2,128,128]{4,3,2,1,0:T(8,128)(2,1)S(1)} %collective-permute-done.10.refs_2_), channel_id=1, source_target_pairs={{0,1},{1,0},{2,3},{3,2},{4,5},{5,4},{6,7},{7,6},{8,9},{9,8},{10,11... | collective-permute-start | bytes 1572872 | tf_op jit(solution)/shard_map/ppermute | solution.py:338
  40.3 0.8 copy-start.15
  41.8 17.8 %collective-permute-start.12 = (bf16[4,2,2,128,128]{4,3,2,1,0:T(8,128)(2,1)S(1)}, bf16[4,2,2,128,128]{4,3,2,1,0:T(8,128)(2,1)S(1)}, u32[]{:S(2)}, u32[]{:S(2)}) collective-permute-start(bf16[4,2,2,128,128]{4,3,2,1,0:T(8,128)(2,1)S(1)} %collective-permute-done.9.refs_2_), channel_id=1, source_target_pairs={{0,1},{1,0},{2,3},{3,2},{4,5},{5,4},{6,7},{7,6},{8,9},{9,8},{10,11... | collective-permute-start | bytes 1572872 | tf_op jit(solution)/shard_map/ppermute | solution.py:338
  41.9 17.7 %copy-start.9 = (bf16[4,2,2,128,128]{4,3,2,1,0:T(8,128)(2,1)}, bf16[4,2,2,128,128]{4,3,2,1,0:T(8,128)(2,1)S(1)}, u32[]{:S(2)}) copy-start(bf16[4,2,2,128,128]{4,3,2,1,0:T(8,128)(2,1)S(1)} %collective-permute-done.11.refs_3_) | copy-start | bytes 1572868
  41.9 19.8 %collective-permute-start.13 = (bf16[4,2,2,128,128]{4,3,2,1,0:T(8,128)(2,1)S(1)}, bf16[4,2,2,128,128]{4,3,2,1,0:T(8,128)(2,1)S(1)}, u32[]{:S(2)}, u32[]{:S(2)}) collective-permute-start(bf16[4,2,2,128,128]{4,3,2,1,0:T(8,128)(2,1)S(1)} %collective-permute-done.11.refs_3_), channel_id=1, source_target_pairs={{0,1},{1,0},{2,3},{3,2},{4,5},{5,4},{6,7},{7,6},{8,9},{9,8},{10,11... | collective-permute-start | bytes 1572872 | tf_op jit(solution)/shard_map/ppermute | solution.py:338
  48.7 36.4 %collective-permute-start.2 = (bf16[8,2,128,128]{3,2,1,0:T(8,128)(2,1)S(1)}, bf16[8,2,128,128]{3,2,1,0:T(8,128)(2,1)S(1)}, u32[]{:S(2)}, u32[]{:S(2)}) collective-permute-start(bf16[8,2,128,128]{3,2,1,0:T(8,128)(2,1)S(1)} %collective-permute-done.1.refs_1_), channel_id=1, source_target_pairs={{16,20},{20,16},{24,28},{28,24},{17,21},{21,17},{25,29},{29,25},{1... | collective-permute-start | bytes 1572872 | tf_op jit(solution)/shard_map/ppermute | solution.py:338
  55.4 0.8 copy-start.17
  56.2 28.9 %collective-permute-start.17 = (bf16[4,2,128,128]{3,2,1,0:T(8,128)(2,1)}, bf16[4,2,128,128]{3,2,1,0:T(8,128)(2,1)}, u32[]{:S(2)}, u32[]{:S(2)}) collective-permute-start(bf16[4,2,128,128]{3,2,1,0:T(8,128)(2,1)} %slice.18), channel_id=1, source_target_pairs={{8,24},{12,28},{9,25},{13,29},{10,26},{14,30},{11,27},{15,31}} | collective-permute-start | bytes 786440 | tf_op jit(solution)/shard_map/ppermute | solution.py:338
  57.5 0.8 copy-start.19
  58.3 26.8 %collective-permute-start.18 = (bf16[4,2,128,128]{3,2,1,0:T(8,128)(2,1)}, bf16[4,2,128,128]{3,2,1,0:T(8,128)(2,1)}, u32[]{:S(2)}, u32[]{:S(2)}) collective-permute-start(bf16[4,2,128,128]{3,2,1,0:T(8,128)(2,1)} %get-tuple-element.9), channel_id=1, source_target_pairs={{8,24},{12,28},{9,25},{13,29},{10,26},{14,30},{11,27},{15,31}} | collective-permute-start | bytes 786440 | tf_op jit(solution)/shard_map/ppermute | solution.py:338
  59.6 0.8 copy-start.11
  60.4 28.0 %collective-permute-start.5 = (bf16[4,2,128,128]{3,2,1,0:T(8,128)(2,1)}, bf16[4,2,128,128]{3,2,1,0:T(8,128)(2,1)}, u32[]{:S(2)}, u32[]{:S(2)}) collective-permute-start(bf16[4,2,128,128]{3,2,1,0:T(8,128)(2,1)} %get-tuple-element.10), channel_id=1, source_target_pairs={{8,24},{12,28},{9,25},{13,29},{10,26},{14,30},{11,27},{15,31}} | collective-permute-start | bytes 786440 | tf_op jit(solution)/shard_map/ppermute | solution.py:338
  61.7 0.8 copy-start.13
  62.5 25.9 %collective-permute-start.3 = (bf16[4,2,128,128]{3,2,1,0:T(8,128)(2,1)}, bf16[4,2,128,128]{3,2,1,0:T(8,128)(2,1)}, u32[]{:S(2)}, u32[]{:S(2)}) collective-permute-start(bf16[4,2,128,128]{3,2,1,0:T(8,128)(2,1)} %slice.16), channel_id=1, source_target_pairs={{16,24},{20,28},{17,25},{21,29},{18,26},{22,30},{19,27},{23,31}} | collective-permute-start | bytes 786440 | tf_op jit(solution)/shard_map/ppermute | solution.py:338
  63.8 6.4 %copy-start.2 = (bf16[8,2,128,128]{3,2,1,0:T(8,128)(2,1)S(1)}, bf16[8,2,128,128]{3,2,1,0:T(8,128)(2,1)}, u32[]{:S(2)}) copy-start(bf16[8,2,128,128]{3,2,1,0:T(8,128)(2,1)} %copy-done.1) | copy-start | bytes 1572868
  64.6 1.0 %copy-start.4 = (bf16[8,2,128,128]{3,2,1,0:T(8,128)(2,1)S(1)}, bf16[8,2,128,128]{3,2,1,0:T(8,128)(2,1)}, u32[]{:S(2)}) copy-start(bf16[8,2,128,128]{3,2,1,0:T(8,128)(2,1)} %copy-done.3) | copy-start | bytes 1572868
  65.6 1.0 %copy-start.8 = (bf16[8,2,128,128]{3,2,1,0:T(8,128)(2,1)S(1)}, bf16[8,2,128,128]{3,2,1,0:T(8,128)(2,1)}, u32[]{:S(2)}) copy-start(bf16[8,2,128,128]{3,2,1,0:T(8,128)(2,1)} %copy-done.7) | copy-start | bytes 1572868
  66.7 3.5 %copy-start.16 = (bf16[4,2,2,128,128]{4,3,2,1,0:T(8,128)(2,1)S(1)}, bf16[4,2,2,128,128]{4,3,2,1,0:T(8,128)(2,1)}, u32[]{:S(2)}) copy-start(bf16[4,2,2,128,128]{4,3,2,1,0:T(8,128)(2,1)} %copy-done.15) | copy-start | bytes 1572868
  66.7 3.5 %copy-start.18 = (bf16[4,2,2,128,128]{4,3,2,1,0:T(8,128)(2,1)S(1)}, bf16[4,2,2,128,128]{4,3,2,1,0:T(8,128)(2,1)}, u32[]{:S(2)}) copy-start(bf16[4,2,2,128,128]{4,3,2,1,0:T(8,128)(2,1)} %copy-done.17) | copy-start | bytes 1572868
  66.7 3.5 %copy-start.20 = (bf16[4,2,2,128,128]{4,3,2,1,0:T(8,128)(2,1)S(1)}, bf16[4,2,2,128,128]{4,3,2,1,0:T(8,128)(2,1)}, u32[]{:S(2)}) copy-start(bf16[4,2,2,128,128]{4,3,2,1,0:T(8,128)(2,1)} %copy-done.19) | copy-start | bytes 1572868
  70.2 7.2 %copy-start.6 = (bf16[4,2,2,128,128]{4,3,2,1,0:T(8,128)(2,1)S(1)}, bf16[4,2,2,128,128]{4,3,2,1,0:T(8,128)(2,1)}, u32[]{:S(2)}) copy-start(bf16[4,2,2,128,128]{4,3,2,1,0:T(8,128)(2,1)} %copy-done.5) | copy-start | bytes 1572868
  70.2 7.2 %copy-start.10 = (bf16[4,2,2,128,128]{4,3,2,1,0:T(8,128)(2,1)S(1)}, bf16[4,2,2,128,128]{4,3,2,1,0:T(8,128)(2,1)}, u32[]{:S(2)}) copy-start(bf16[4,2,2,128,128]{4,3,2,1,0:T(8,128)(2,1)} %copy-done.9) | copy-start | bytes 1572868
  70.2 7.2 %copy-start.12 = (bf16[4,2,2,128,128]{4,3,2,1,0:T(8,128)(2,1)S(1)}, bf16[4,2,2,128,128]{4,3,2,1,0:T(8,128)(2,1)}, u32[]{:S(2)}) copy-start(bf16[4,2,2,128,128]{4,3,2,1,0:T(8,128)(2,1)} %copy-done.11) | copy-start | bytes 1572868
  70.2 7.2 %copy-start.14 = (bf16[4,2,2,128,128]{4,3,2,1,0:T(8,128)(2,1)S(1)}, bf16[4,2,2,128,128]{4,3,2,1,0:T(8,128)(2,1)}, u32[]{:S(2)}) copy-start(bf16[4,2,2,128,128]{4,3,2,1,0:T(8,128)(2,1)} %copy-done.13) | copy-start | bytes 1572868
